TPU v7x, 256 devices: a whole 4x4x8 slice. The times are simulated.
256 devices in a mesh: gx: 4 (over z_hi), gy: 4 (over y), gz: 16 (over x, z_lo, core).
Axes of the slice: x: 4, y: 4, z: 8 (z_hi: 4, z_lo: 2; z = z_hi * 2 + z_lo), core: 2. Of those that a mesh axis runs over, the one named last changes fastest.
Arguments:
- volume: float32 [256, 256, 4096], P('gz', 'gy', 'gx'), may hold values from -24 to 24
Outputs:
- level_one: float32 [128, 128, 2048], P('gz', 'gy', 'gx')
- level_two: float32 [64, 64, 1024], P('gz', 'gy', 'gx')
- level_three: float32 [32, 32, 512], P('gz', 'gy', 'gx')
All inputs are finite; a program needn't handle non-finite values.
Results may differ from a plain program's by a relative error of at most 0.00002.
Values sent between devices are 32-bit elements; how exact they have to be, the bound alone decides.
A program may use at most 64 MiB of HBM per device.

v0:
```python
import jax
import jax.numpy as jnp
from jax import lax
from jax.sharding import PartitionSpec as P

taps = (0.0625, 0.25, 0.375, 0.25, 0.0625)


def extended(cells, sides, width):
    for axis, dim in sides:
        count = lax.axis_size(axis)
        ends = count - 1
        head = lax.slice_in_dim(cells, 0, width, axis=dim)
        tail = lax.slice_in_dim(cells, cells.shape[dim] - width, cells.shape[dim], axis=dim)
        cells = jnp.concatenate(
            [
                lax.ppermute(tail, axis, [(i, (i + 1) % count) for i in range(ends)]),
                cells,
                lax.ppermute(head, axis, [((i + 1) % count, i) for i in range(ends)]),
            ],
            axis=dim,
        )
    return cells


def reduce_padded(padded, dim, count):
    total = None
    for k in range(5):
        piece = lax.slice_in_dim(padded, k, k + 2 * count - 1, 2, dim)
        term = taps[k] * piece
        total = term if total is None else total + term
    return total


def pass_sections(block):
    padded = extended(block, (("gz", 0),), 2)
    return reduce_padded(padded, 0, block.shape[0] // 2)


def pass_rows(block):
    padded = extended(block, (("gy", 1),), 2)
    return reduce_padded(padded, 1, block.shape[1] // 2)


def pass_columns(block):
    padded = extended(block, (("gx", 2),), 2)
    return reduce_padded(padded, 2, block.shape[2] // 2)


def level_down(block):
    return pass_columns(pass_rows(pass_sections(block)))


def on_device(volume):
    level_one = level_down(volume)
    level_two = level_down(level_one)
    level_three = level_down(level_two)
    return (level_one, level_two, level_three)


def solution(mesh):
    in_specs = (P("gz", "gy", "gx"),)
    out_specs = (P("gz", "gy", "gx"), P("gz", "gy", "gx"), P("gz", "gy", "gx"))
    return jax.shard_map(
        on_device, mesh=mesh, in_specs=in_specs, out_specs=out_specs, check_vma=False
    )
```

profile of v0, /device:TPU:66, one launch (start us, length us, event | category | flops | bytes accessed | tf_op | source)
XLA Modules:
  0.0 221.4 jit_solution(7761092275039604067)
XLA Ops:
  0.6 1.3 fusion
  1.9 1.9 collective-permute-start
  3.9 4.5 %collective-permute-start.1 = (f32[2,64,1024]{2,1,0:T(8,128)S(1)}, f32[2,64,1024]{2,1,0:T(8,128)S(1)}, u32[]{:S(2)}, u32[]{:S(2)}) collective-permute-start(f32[2,64,1024]{2,1,0:T(8,128)S(1)} %get-tuple-element.3), channel_id=1, source_target_pairs={{1,0},{2,1},{3,2},{4,3},{5,4},{6,5},{7,6},{8,7},{9,8},{10,9},{11,1... | collective-permute-start | bytes 1572872 | tf_op jit(solution)/shard_map/ppermute | solution.py:19
  8.4 7.3 %collective-permute-done = f32[2,64,1024]{2,1,0:T(8,128)S(1)} collective-permute-done((f32[2,64,1024]{2,1,0:T(8,128)S(1)}, f32[2,64,1024]{2,1,0:T(8,128)S(1)}, u32[]{:S(2)}, u32[]{:S(2)}) %collective-permute-start) | collective-permute-done | bytes 524320 | tf_op jit(solution)/shard_map/ppermute | solution.py:17
  15.8 2.7 %constant_dynamic-update-slice_fusion.1 = f32[20,64,1024]{2,1,0:T(8,128)S(1)} fusion(f32[20,64,1024]{2,1,0:T(8,128)S(1)} %constant_dynamic-update-slice_fusion.2, f32[16,64,1024]{2,1,0:T(8,128)} %param.1), kind=kLoop, calls=%fused_computation.16 | loop fusion | bytes 8388608
  18.5 0.7 copy-done
  19.2 1.1 multiply_add_fusion
  20.4 3.5 %collective-permute-start.2 = (f32[8,2,1024]{2,1,0:T(2,128)S(1)}, f32[8,2,1024]{2,1,0:T(2,128)S(1)}, u32[]{:S(2)}, u32[]{:S(2)}) collective-permute-start(f32[8,2,1024]{2,1,0:T(2,128)S(1)} %get-tuple-element.5), channel_id=1, source_target_pairs={{0,16},{16,32},{32,48},{1,17},{17,33},{33,49},{2,18},{18,34},{34,5... | collective-permute-start | bytes 196616 | tf_op jit(solution)/shard_map/ppermute | solution.py:17
  23.8 1.3 collective-permute-start.3
  25.1 0.5 slice.200
  25.6 2.8 %slice.201 = f32[8,32,1024]{2,1,0:T(8,128)} slice(f32[8,64,1024]{2,1,0:T(8,128)S(1)} %multiply_add_fusion), slice={[0:8:1], [1:64:2], [0:1024:1]} | slice | bytes 2097152 | tf_op jit(solution)/shard_map/slice | solution.py:29
  28.5 1.5 collective-permute-done.3
  30.0 1.7 pad_maximum_fusion
  31.8 5.5 %slice.202 = f32[8,32,1024]{2,1,0:T(8,128)} slice(f32[8,68,1024]{2,1,0:T(8,128)} %pad_maximum_fusion), slice={[0:8:1], [4:67:2], [0:1024:1]} | slice | bytes 2097152 | tf_op jit(solution)/shard_map/slice | solution.py:29
  37.2 5.5 %slice.199 = f32[8,32,1024]{2,1,0:T(8,128)} slice(f32[8,68,1024]{2,1,0:T(8,128)} %pad_maximum_fusion), slice={[0:8:1], [1:64:2], [0:1024:1]} | slice | bytes 2097152 | tf_op jit(solution)/shard_map/slice | solution.py:29
  42.8 5.4 %slice.198 = f32[8,32,1024]{2,1,0:T(8,128)} slice(f32[8,68,1024]{2,1,0:T(8,128)} %pad_maximum_fusion), slice={[0:8:1], [0:63:2], [0:1024:1]} | slice | bytes 2097152 | tf_op jit(solution)/shard_map/slice | solution.py:29
  48.1 2.4 %multiply_add_fusion.1 = f32[8,32,1024]{2,1,0:T(8,128)S(1)} fusion(f32[8,32,1024]{2,1,0:T(8,128)} %slice.202, f32[8,32,1024]{2,1,0:T(8,128)S(1)} %copy-done.2, f32[8,32,1024]{2,1,0:T(8,128)S(1)} %slice.200, f32[8,32,1024]{2,1,0:T(8,128)} %slice.199, f32[8,32,1024]{2,1,0:T(8,128)} %slice.198), kind=kLoop, calls=%fused_computation.2 | loop fusion | flops 2359296 | bytes 6291456 | tf_op jit(solution)/shard_map/add | solution.py:31
  50.6 0.1 fusion.2
  50.7 1.9 collective-permute-start.5
  52.6 7.5 %collective-permute-start.4 = (f32[8,32,2]{2,1,0:T(8,128)S(1)}, f32[8,32,2]{2,1,0:T(8,128)S(1)}, u32[]{:S(2)}, u32[]{:S(2)}) collective-permute-start(f32[8,32,2]{2,1,0:T(8,128)S(1)} %get-tuple-element.8), channel_id=1, source_target_pairs={{0,64},{64,128},{128,192},{1,65},{65,129},{129,193},{2,66},{66,130... | collective-permute-start | bytes 6152 | tf_op jit(solution)/shard_map/ppermute | solution.py:17
  60.1 17.6 %slice.207 = f32[8,32,512]{2,1,0:T(8,128)S(1)} slice(f32[8,32,1024]{2,1,0:T(8,128)S(1)} %multiply_add_fusion.1), slice={[0:8:1], [0:32:1], [0:1023:2]} | slice | bytes 1048576 | tf_op jit(solution)/shard_map/slice | solution.py:29
  77.7 17.6 %slice.208 = f32[8,32,512]{2,1,0:T(8,128)S(1)} slice(f32[8,32,1024]{2,1,0:T(8,128)S(1)} %multiply_add_fusion.1), slice={[0:8:1], [0:32:1], [1:1024:2]} | slice | bytes 1048576 | tf_op jit(solution)/shard_map/slice | solution.py:29
  95.3 0.8 concatenate.29
  96.1 17.6 %slice.209 = f32[8,32,512]{2,1,0:T(8,128)S(1)} slice(f32[8,32,1028]{2,1,0:T(8,128)S(1)} %concatenate.29), slice={[0:8:1], [0:32:1], [4:1027:2]} | slice | bytes 1048576 | tf_op jit(solution)/shard_map/slice | solution.py:29
  113.7 18.4 %slice.206 = f32[8,32,512]{2,1,0:T(8,128)} slice(f32[8,32,1028]{2,1,0:T(8,128)S(1)} %concatenate.29), slice={[0:8:1], [0:32:1], [1:1024:2]} | slice | bytes 1048576 | tf_op jit(solution)/shard_map/slice | solution.py:29
  132.0 18.2 %slice.205 = f32[8,32,512]{2,1,0:T(8,128)} slice(f32[8,32,1028]{2,1,0:T(8,128)S(1)} %concatenate.29), slice={[0:8:1], [0:32:1], [0:1023:2]} | slice | bytes 1048576 | tf_op jit(solution)/shard_map/slice | solution.py:29
  150.2 1.5 multiply_add_fusion.2
  151.7 1.9 collective-permute-start.6
  153.7 4.5 %collective-permute-start.7 = (f32[2,32,512]{2,1,0:T(8,128)S(1)}, f32[2,32,512]{2,1,0:T(8,128)S(1)}, u32[]{:S(2)}, u32[]{:S(2)}) collective-permute-start(f32[2,32,512]{2,1,0:T(8,128)S(1)} %get-tuple-element.10), channel_id=1, source_target_pairs={{1,0},{2,1},{3,2},{4,3},{5,4},{6,5},{7,6},{8,7},{9,8},{10,9},{11,1... | collective-permute-start | bytes 393224 | tf_op jit(solution)/shard_map/ppermute | solution.py:19
  158.2 1.7 collective-permute-done.6
  159.9 0.8 collective-permute-done.7
  160.7 0.1 pad_maximum_fusion.1
  160.8 0.1 multiply_add_fusion.3
  160.9 3.5 %collective-permute-start.8 = (f32[4,2,512]{2,1,0:T(2,128)S(1)}, f32[4,2,512]{2,1,0:T(2,128)S(1)}, u32[]{:S(2)}, u32[]{:S(2)}) collective-permute-start(f32[4,2,512]{2,1,0:T(2,128)S(1)} %get-tuple-element.11), channel_id=1, source_target_pairs={{0,16},{16,32},{32,48},{1,17},{17,33},{33,49},{2,18},{18,34},{34,5... | collective-permute-start | bytes 49160 | tf_op jit(solution)/shard_map/ppermute | solution.py:17
  164.4 1.3 collective-permute-start.9
  165.9 4.2 %collective-permute-done.9 = f32[4,2,512]{2,1,0:T(2,128)S(1)} collective-permute-done((f32[4,2,512]{2,1,0:T(2,128)S(1)}, f32[4,2,512]{2,1,0:T(2,128)S(1)}, u32[]{:S(2)}, u32[]{:S(2)}) %collective-permute-start.9) | collective-permute-done | bytes 16416 | tf_op jit(solution)/shard_map/ppermute | solution.py:19
  170.1 0.1 slice.223
  170.3 0.1 fusion.5
  170.4 4.8 %collective-permute-start.10 = (f32[4,16,2]{2,1,0:T(8,128)S(1)}, f32[4,16,2]{2,1,0:T(8,128)S(1)}, u32[]{:S(2)}, u32[]{:S(2)}) collective-permute-start(f32[4,16,2]{2,1,0:T(8,128)S(1)} %get-tuple-element.13), channel_id=1, source_target_pairs={{0,64},{64,128},{128,192},{1,65},{65,129},{129,193},{2,66},{66,130... | collective-permute-start | bytes 1544 | tf_op jit(solution)/shard_map/ppermute | solution.py:17
  175.2 2.2 collective-permute-start.11
  177.4 2.2 slice.228
  179.7 2.2 slice.229
  181.9 1.6 collective-permute-done.11
  183.5 0.1 pad_maximum_fusion.3
  183.6 2.2 %slice.230 = f32[4,16,256]{2,1,0:T(8,128)S(1)} slice(f32[4,16,516]{2,1,0:T(8,128)S(1)} %pad_maximum_fusion.3), slice={[0:4:1], [0:16:1], [4:515:2]} | slice | bytes 131072 | tf_op jit(solution)/shard_map/slice | solution.py:29
  185.8 2.2 slice.227
  188.0 2.2 slice.226
  190.3 1.9 collective-permute-start.12
  192.2 4.5 %collective-permute-start.13 = (f32[2,16,256]{2,1,0:T(8,128)S(1)}, f32[2,16,256]{2,1,0:T(8,128)S(1)}, u32[]{:S(2)}, u32[]{:S(2)}) collective-permute-start(f32[2,16,256]{2,1,0:T(8,128)S(1)} %get-tuple-element.16), channel_id=1, source_target_pairs={{1,0},{2,1},{3,2},{4,3},{5,4},{6,5},{7,6},{8,7},{9,8},{10,9},{11,1... | collective-permute-start | bytes 98312 | tf_op jit(solution)/shard_map/ppermute | solution.py:19
  196.8 1.6 collective-permute-done.13
  198.4 3.2 %collective-permute-start.14 = (f32[2,2,256]{2,1,0:T(2,128)S(1)}, f32[2,2,256]{2,1,0:T(2,128)S(1)}, u32[]{:S(2)}, u32[]{:S(2)}) collective-permute-start(f32[2,2,256]{2,1,0:T(2,128)S(1)} %get-tuple-element.17), channel_id=1, source_target_pairs={{0,16},{16,32},{32,48},{1,17},{17,33},{33,49},{2,18},{18,34},{34,5... | collective-permute-start | bytes 12296 | tf_op jit(solution)/shard_map/ppermute | solution.py:17
  201.6 1.3 collective-permute-start.15
  202.9 4.2 %collective-permute-done.15 = f32[2,2,256]{2,1,0:T(2,128)S(1)} collective-permute-done((f32[2,2,256]{2,1,0:T(2,128)S(1)}, f32[2,2,256]{2,1,0:T(2,128)S(1)}, u32[]{:S(2)}, u32[]{:S(2)}) %collective-permute-start.15) | collective-permute-done | bytes 4128 | tf_op jit(solution)/shard_map/ppermute | solution.py:19
  207.2 0.3 slice.249
  207.5 0.1 fusion.8
  207.6 4.5 %collective-permute-start.16 = (f32[2,8,2]{2,1,0:T(8,128)S(1)}, f32[2,8,2]{2,1,0:T(8,128)S(1)}, u32[]{:S(2)}, u32[]{:S(2)}) collective-permute-start(f32[2,8,2]{2,1,0:T(8,128)S(1)} %get-tuple-element.19), channel_id=1, source_target_pairs={{0,64},{64,128},{128,192},{1,65},{65,129},{129,193},{2,66},{66,130... | collective-permute-start | bytes 392 | tf_op jit(solution)/shard_map/ppermute | solution.py:17
  212.1 2.3 %collective-permute-start.17 = (f32[2,8,2]{2,1,0:T(8,128)S(1)}, f32[2,8,2]{2,1,0:T(8,128)S(1)}, u32[]{:S(2)}, u32[]{:S(2)}) collective-permute-start(f32[2,8,2]{2,1,0:T(8,128)S(1)} %get-tuple-element.20), channel_id=1, source_target_pairs={{64,0},{128,64},{192,128},{65,1},{129,65},{193,129},{66,2},{130,66... | collective-permute-start | bytes 392 | tf_op jit(solution)/shard_map/ppermute | solution.py:19
  214.4 0.3 slice.250
  214.7 5.0 %collective-permute-done.17 = f32[2,8,2]{2,1,0:T(8,128)S(1)} collective-permute-done((f32[2,8,2]{2,1,0:T(8,128)S(1)}, f32[2,8,2]{2,1,0:T(8,128)S(1)}, u32[]{:S(2)}, u32[]{:S(2)}) %collective-permute-start.17) | collective-permute-done | bytes 160 | tf_op jit(solution)/shard_map/ppermute | solution.py:19
  219.7 0.1 pad_maximum_fusion.6
  219.8 0.3 slice.251
  220.1 0.3 slice.248
  220.5 0.3 slice.247
  220.8 0.6 multiply_add_fusion.8
  (39 shorter events, 0.7 us)
Async XLA Ops:
  1.9 13.8 %collective-permute-start = (f32[2,64,1024]{2,1,0:T(8,128)S(1)}, f32[2,64,1024]{2,1,0:T(8,128)S(1)}, u32[]{:S(2)}, u32[]{:S(2)}) collective-permute-start(f32[2,64,1024]{2,1,0:T(8,128)S(1)} %get-tuple-element.4), channel_id=1, source_target_pairs={{0,1},{1,2},{2,3},{3,4},{4,5},{5,6},{6,7},{7,8},{8,9},{9,10},{10,1... | collective-permute-start | bytes 1572872 | tf_op jit(solution)/shard_map/ppermute | solution.py:17
  3.9 14.6 %collective-permute-start.1 = (f32[2,64,1024]{2,1,0:T(8,128)S(1)}, f32[2,64,1024]{2,1,0:T(8,128)S(1)}, u32[]{:S(2)}, u32[]{:S(2)}) collective-permute-start(f32[2,64,1024]{2,1,0:T(8,128)S(1)} %get-tuple-element.3), channel_id=1, source_target_pairs={{1,0},{2,1},{3,2},{4,3},{5,4},{6,5},{7,6},{8,7},{9,8},{10,9},{11,1... | collective-permute-start | bytes 1572872 | tf_op jit(solution)/shard_map/ppermute | solution.py:19
  15.8 3.5 %copy-start = (f32[16,64,1024]{2,1,0:T(8,128)S(1)}, f32[16,64,1024]{2,1,0:T(8,128)}, u32[]{:S(2)}) copy-start(f32[16,64,1024]{2,1,0:T(8,128)} %param.1) | copy-start | bytes 12582916
  20.4 8.1 %collective-permute-start.2 = (f32[8,2,1024]{2,1,0:T(2,128)S(1)}, f32[8,2,1024]{2,1,0:T(2,128)S(1)}, u32[]{:S(2)}, u32[]{:S(2)}) collective-permute-start(f32[8,2,1024]{2,1,0:T(2,128)S(1)} %get-tuple-element.5), channel_id=1, source_target_pairs={{0,16},{16,32},{32,48},{1,17},{17,33},{33,49},{2,18},{18,34},{34,5... | collective-permute-start | bytes 196616 | tf_op jit(solution)/shard_map/ppermute | solution.py:17
  23.8 6.2 %collective-permute-start.3 = (f32[8,2,1024]{2,1,0:T(2,128)S(1)}, f32[8,2,1024]{2,1,0:T(2,128)S(1)}, u32[]{:S(2)}, u32[]{:S(2)}) collective-permute-start(f32[8,2,1024]{2,1,0:T(2,128)S(1)} %get-tuple-element.6), channel_id=1, source_target_pairs={{16,0},{32,16},{48,32},{17,1},{33,17},{49,33},{18,2},{34,18},{50,3... | collective-permute-start | bytes 196616 | tf_op jit(solution)/shard_map/ppermute | solution.py:19
  37.2 10.9 %copy-start.2 = (f32[8,32,1024]{2,1,0:T(8,128)S(1)}, f32[8,32,1024]{2,1,0:T(8,128)}, u32[]{:S(2)}) copy-start(f32[8,32,1024]{2,1,0:T(8,128)} %slice.201) | copy-start | bytes 3145732
  50.7 44.6 %collective-permute-start.5 = (f32[8,32,2]{2,1,0:T(8,128)S(1)}, f32[8,32,2]{2,1,0:T(8,128)S(1)}, u32[]{:S(2)}, u32[]{:S(2)}) collective-permute-start(f32[8,32,2]{2,1,0:T(8,128)S(1)} %get-tuple-element.7), channel_id=1, source_target_pairs={{64,0},{128,64},{192,128},{65,1},{129,65},{193,129},{66,2},{130,66... | collective-permute-start | bytes 6152 | tf_op jit(solution)/shard_map/ppermute | solution.py:19
  52.6 42.6 %collective-permute-start.4 = (f32[8,32,2]{2,1,0:T(8,128)S(1)}, f32[8,32,2]{2,1,0:T(8,128)S(1)}, u32[]{:S(2)}, u32[]{:S(2)}) collective-permute-start(f32[8,32,2]{2,1,0:T(8,128)S(1)} %get-tuple-element.8), channel_id=1, source_target_pairs={{0,64},{64,128},{128,192},{1,65},{65,129},{129,193},{2,66},{66,130... | collective-permute-start | bytes 6152 | tf_op jit(solution)/shard_map/ppermute | solution.py:17
  151.7 14.1 %copy-start.1 = (f32[8,32,512]{2,1,0:T(8,128)}, f32[8,32,512]{2,1,0:T(8,128)S(1)}, u32[]{:S(2)}) copy-start(f32[8,32,512]{2,1,0:T(8,128)S(1)} %multiply_add_fusion.2) | copy-start | bytes 1572868
  151.7 8.2 %collective-permute-start.6 = (f32[2,32,512]{2,1,0:T(8,128)S(1)}, f32[2,32,512]{2,1,0:T(8,128)S(1)}, u32[]{:S(2)}, u32[]{:S(2)}) collective-permute-start(f32[2,32,512]{2,1,0:T(8,128)S(1)} %get-tuple-element.9), channel_id=1, source_target_pairs={{0,1},{1,2},{2,3},{3,4},{4,5},{5,6},{6,7},{7,8},{8,9},{9,10},{10,1... | collective-permute-start | bytes 393224 | tf_op jit(solution)/shard_map/ppermute | solution.py:17
  153.7 7.0 %collective-permute-start.7 = (f32[2,32,512]{2,1,0:T(8,128)S(1)}, f32[2,32,512]{2,1,0:T(8,128)S(1)}, u32[]{:S(2)}, u32[]{:S(2)}) collective-permute-start(f32[2,32,512]{2,1,0:T(8,128)S(1)} %get-tuple-element.10), channel_id=1, source_target_pairs={{1,0},{2,1},{3,2},{4,3},{5,4},{6,5},{7,6},{8,7},{9,8},{10,9},{11,1... | collective-permute-start | bytes 393224 | tf_op jit(solution)/shard_map/ppermute | solution.py:19
  160.9 4.9 %collective-permute-start.8 = (f32[4,2,512]{2,1,0:T(2,128)S(1)}, f32[4,2,512]{2,1,0:T(2,128)S(1)}, u32[]{:S(2)}, u32[]{:S(2)}) collective-permute-start(f32[4,2,512]{2,1,0:T(2,128)S(1)} %get-tuple-element.11), channel_id=1, source_target_pairs={{0,16},{16,32},{32,48},{1,17},{17,33},{33,49},{2,18},{18,34},{34,5... | collective-permute-start | bytes 49160 | tf_op jit(solution)/shard_map/ppermute | solution.py:17
  164.4 5.6 %collective-permute-start.9 = (f32[4,2,512]{2,1,0:T(2,128)S(1)}, f32[4,2,512]{2,1,0:T(2,128)S(1)}, u32[]{:S(2)}, u32[]{:S(2)}) collective-permute-start(f32[4,2,512]{2,1,0:T(2,128)S(1)} %get-tuple-element.12), channel_id=1, source_target_pairs={{16,0},{32,16},{48,32},{17,1},{33,17},{49,33},{18,2},{34,18},{50,3... | collective-permute-start | bytes 49160 | tf_op jit(solution)/shard_map/ppermute | solution.py:19
  170.4 11.4 %collective-permute-start.10 = (f32[4,16,2]{2,1,0:T(8,128)S(1)}, f32[4,16,2]{2,1,0:T(8,128)S(1)}, u32[]{:S(2)}, u32[]{:S(2)}) collective-permute-start(f32[4,16,2]{2,1,0:T(8,128)S(1)} %get-tuple-element.13), channel_id=1, source_target_pairs={{0,64},{64,128},{128,192},{1,65},{65,129},{129,193},{2,66},{66,130... | collective-permute-start | bytes 1544 | tf_op jit(solution)/shard_map/ppermute | solution.py:17
  175.2 8.2 %collective-permute-start.11 = (f32[4,16,2]{2,1,0:T(8,128)S(1)}, f32[4,16,2]{2,1,0:T(8,128)S(1)}, u32[]{:S(2)}, u32[]{:S(2)}) collective-permute-start(f32[4,16,2]{2,1,0:T(8,128)S(1)} %get-tuple-element.14), channel_id=1, source_target_pairs={{64,0},{128,64},{192,128},{65,1},{129,65},{193,129},{66,2},{130,66... | collective-permute-start | bytes 1544 | tf_op jit(solution)/shard_map/ppermute | solution.py:19
  190.3 31.2 %copy-start.3 = (f32[4,16,256]{2,1,0:T(8,128)}, f32[4,16,256]{2,1,0:T(8,128)S(1)}, u32[]{:S(2)}) copy-start(f32[4,16,256]{2,1,0:T(8,128)S(1)} %multiply_add_fusion.5) | copy-start | bytes 196612
  190.3 6.5 %collective-permute-start.12 = (f32[2,16,256]{2,1,0:T(8,128)S(1)}, f32[2,16,256]{2,1,0:T(8,128)S(1)}, u32[]{:S(2)}, u32[]{:S(2)}) collective-permute-start(f32[2,16,256]{2,1,0:T(8,128)S(1)} %get-tuple-element.15), channel_id=1, source_target_pairs={{0,1},{1,2},{2,3},{3,4},{4,5},{5,6},{6,7},{7,8},{8,9},{9,10},{10,1... | collective-permute-start | bytes 98312 | tf_op jit(solution)/shard_map/ppermute | solution.py:17
  192.2 6.1 %collective-permute-start.13 = (f32[2,16,256]{2,1,0:T(8,128)S(1)}, f32[2,16,256]{2,1,0:T(8,128)S(1)}, u32[]{:S(2)}, u32[]{:S(2)}) collective-permute-start(f32[2,16,256]{2,1,0:T(8,128)S(1)} %get-tuple-element.16), channel_id=1, source_target_pairs={{1,0},{2,1},{3,2},{4,3},{5,4},{6,5},{7,6},{8,7},{9,8},{10,9},{11,1... | collective-permute-start | bytes 98312 | tf_op jit(solution)/shard_map/ppermute | solution.py:19
  198.4 4.5 %collective-permute-start.14 = (f32[2,2,256]{2,1,0:T(2,128)S(1)}, f32[2,2,256]{2,1,0:T(2,128)S(1)}, u32[]{:S(2)}, u32[]{:S(2)}) collective-permute-start(f32[2,2,256]{2,1,0:T(2,128)S(1)} %get-tuple-element.17), channel_id=1, source_target_pairs={{0,16},{16,32},{32,48},{1,17},{17,33},{33,49},{2,18},{18,34},{34,5... | collective-permute-start | bytes 12296 | tf_op jit(solution)/shard_map/ppermute | solution.py:17
  201.6 5.5 %collective-permute-start.15 = (f32[2,2,256]{2,1,0:T(2,128)S(1)}, f32[2,2,256]{2,1,0:T(2,128)S(1)}, u32[]{:S(2)}, u32[]{:S(2)}) collective-permute-start(f32[2,2,256]{2,1,0:T(2,128)S(1)} %get-tuple-element.18), channel_id=1, source_target_pairs={{16,0},{32,16},{48,32},{17,1},{33,17},{49,33},{18,2},{34,18},{50,3... | collective-permute-start | bytes 12296 | tf_op jit(solution)/shard_map/ppermute | solution.py:19
  207.6 7.1 %collective-permute-start.16 = (f32[2,8,2]{2,1,0:T(8,128)S(1)}, f32[2,8,2]{2,1,0:T(8,128)S(1)}, u32[]{:S(2)}, u32[]{:S(2)}) collective-permute-start(f32[2,8,2]{2,1,0:T(8,128)S(1)} %get-tuple-element.19), channel_id=1, source_target_pairs={{0,64},{64,128},{128,192},{1,65},{65,129},{129,193},{2,66},{66,130... | collective-permute-start | bytes 392 | tf_op jit(solution)/shard_map/ppermute | solution.py:17
  212.1 7.7 %collective-permute-start.17 = (f32[2,8,2]{2,1,0:T(8,128)S(1)}, f32[2,8,2]{2,1,0:T(8,128)S(1)}, u32[]{:S(2)}, u32[]{:S(2)}) collective-permute-start(f32[2,8,2]{2,1,0:T(8,128)S(1)} %get-tuple-element.20), channel_id=1, source_target_pairs={{64,0},{128,64},{192,128},{65,1},{129,65},{193,129},{66,2},{130,66... | collective-permute-start | bytes 392 | tf_op jit(solution)/shard_map/ppermute | solution.py:19
where the time goes:
time: 222 us; the launch traced here: 221 us
  local copies, waits for them, and re-layouts  128 us (58%)
  starting transfers between devices  56.5 us (25%)
  waiting for transfers between devices  27.9 us (13%)
  other arithmetic  7.92 us (4%)
    slice x30, local copies, waits for them, and re-layouts, reduce_padded(): piece = lax.slice_in_dim(padded, k, k + 2 * count - 1, 2, dim)  122 us
    ppermute x9, starting transfers between devices, extended(): lax.ppermute(tail, axis, [(i, (i + 1) % count) for i in range(ends)])  32.7 us
    ppermute x9, starting transfers between devices, extended(): lax.ppermute(head, axis, [((i + 1) % count, i) for i in range(ends)])  23.9 us
    ppermute x9, waiting for transfers between devices, extended(): lax.ppermute(head, axis, [((i + 1) % count, i) for i in range(ends)])  18.8 us
    ppermute x9, waiting for transfers between devices, extended(): lax.ppermute(tail, axis, [(i, (i + 1) % count) for i in range(ends)])  9.09 us
    add x9, other arithmetic, reduce_padded(): total = term if total is None else total + term  5.86 us
  transfers between devices with their start and end apart: 18, of which 9 were waited for; matrix products, arithmetic and copies ran while one was open for 21% of the time, Pallas kernels for 0%

commit v1 on v0

v1 whole, which is shorter than its diff:
```python
import functools

import jax
import jax.numpy as jnp
from jax import lax
from jax.experimental import pallas as pl
from jax.experimental.pallas import tpu as pltpu
from jax.sharding import PartitionSpec as P

MESH = pl.DeviceIdType.MESH
F32 = jnp.float32
BF16 = jnp.bfloat16
LANES = 128
taps = (1.0, 4.0, 6.0, 4.0, 1.0)

ROWS1, ROWS2, ROWS3 = 352, 144, 64
PITCH1, PITCH2, PITCH3 = 72, 48, 32
DIRECTIONS = [
    (dz, dy, dx)
    for dx in (1, -1, 0)
    for dz in (1, -1, 0)
    for dy in (1, -1, 0)
    if (dz, dy, dx) != (0, 0, 0)
]
SLOT = {d: i for i, d in enumerate(DIRECTIONS)}
SIDES = [(dz, dy) for dz in (1, -1, 0) for dy in (1, -1, 0) if (dz, dy) != (0, 0)]
SIDE = {d: i for i, d in enumerate(SIDES)}


def weighted(pieces):
    groups = {}
    for k, piece in pieces.items():
        groups.setdefault(taps[k], []).append(piece)
    total = None
    for tap, members in groups.items():
        part = members[0] if len(members) == 1 else members[0] + members[1]
        part = part if tap == 1.0 else tap * part
        total = part if total is None else total + part
    return total


def reduce_planes(load, low, high, out):
    return weighted(
        {k: load(2 * out + k - 2) for k in range(5) if low <= 2 * out + k - 2 <= high}
    )


def split(block):
    first = block.astype(BF16)
    rest = block - first.astype(F32)
    second = rest.astype(BF16)
    third = (rest - second.astype(F32)).astype(BF16)
    return third, second, first


def product(block, weights):
    total = None
    for piece in split(block):
        part = jnp.dot(piece, weights, preferred_element_type=F32)
        total = part if total is None else total + part
    return total


def build_weights(band, edge):
    k = lax.broadcasted_iota(jnp.int32, (256, 256), 0)
    n = lax.broadcasted_iota(jnp.int32, (256, 256), 1)
    out = jnp.where(n < 128, n, jnp.where(n == 128, 128, jnp.where(n == 255, -1, 1000)))
    tap = k - 2 * out + 2
    value = jnp.where(tap == 2, 6.0, jnp.where((tap == 1) | (tap == 3), 4.0, jnp.where((tap == 0) | (tap == 4), 1.0, 0.0)))
    band[...] = (value * (1.0 / 4096.0)).astype(BF16)
    k = lax.broadcasted_iota(jnp.int32, (128, 256), 0)
    n = lax.broadcasted_iota(jnp.int32, (128, 256), 1)
    place = jnp.where(k < 2, k, jnp.where(k == 127, -1, 1000))
    out = jnp.where(n < 2, n, jnp.where(n == 127, -1, jnp.where(n == 255, -1, jnp.where(n == 128, 0, -1000))))
    high_in, low_in = k < 2, k == 127
    high_out = (n < 2) | (n == 255)
    low_out = (n == 127) | (n == 128)
    tap = place - 2 * out + 2
    legal = (high_in & high_out) | (low_in & low_out)
    value = jnp.where(tap == 2, 6.0, jnp.where((tap == 1) | (tap == 3), 4.0, jnp.where((tap == 0) | (tap == 4), 1.0, 0.0)))
    edge[...] = jnp.where(legal, value * (1.0 / 4096.0), 0.0).astype(BF16)


def pyramid(counts, vol, out1, out2, out3, v, zs1, as1, p1, l1, ye1, zs2, as2, p2, l2, ye2, zs3, as3, p3, l3,
            band, edge, xm, xs, rz1, rz2u, rz2d, rz3u, rz3d, ry1, ry2, ry3, rxm, rxs,
            load_sem, send_sem, recv_sem):
    me = {axis: lax.axis_index(axis) for axis in ("gz", "gy", "gx")}
    has = {(axis, 1): me[axis] < counts[axis] - 1 for axis in me}
    has.update({(axis, -1): me[axis] > 0 for axis in me})

    def exists(d):
        ok = None
        for axis, step in zip(("gz", "gy", "gx"), d):
            if step:
                ok = has[axis, step] if ok is None else ok & has[axis, step]
        return ok

    def device(d):
        return {axis: me[axis] + step for axis, step in zip(("gz", "gy", "gx"), d) if step}

    order = (0, 3, 1, 2)
    loads = [
        pltpu.make_async_copy(
            vol.at[:, :, pl.ds(256 * b, 256)], v.at[:, :, pl.ds(256 * b, 256)], load_sem.at[b]
        )
        for b in range(4)
    ]
    for b in order:
        loads[b].start()

    barrier = pltpu.get_barrier_semaphore()
    for d in DIRECTIONS:
        @pl.when(exists(d))
        def _():
            pl.semaphore_signal(barrier, inc=1, device_id=device(d), device_id_type=MESH)

    build_weights(band, edge)
    zero8 = jnp.zeros((8, LANES), F32)
    for c in range(8):
        for p in range(11):
            zs1[c, p * PITCH1:p * PITCH1 + 8, :] = zero8
        as1[c, 328:336, :] = zero8
        as1[c, 344:352, :] = zero8
    for t in range(5):
        for e in range(2):
            for r in range(0, 24, 8):
                ye1[t, e, r:r + 8, :] = zero8
        for p in range(8):
            zs2[t, p * PITCH2:p * PITCH2 + 8, :] = zero8
            zs2[t, p * PITCH2 + 40:p * PITCH2 + 48, :] = zero8
        for r in range(8, 40, 8):
            zs2[t, 7 * PITCH2 + r:7 * PITCH2 + r + 8, :] = zero8
        as2[t, 136:144, :] = zero8
    for t in range(3):
        for e in range(3):
            for r in range(0, 24, 8):
                ye2[t, e, r:r + 8, :] = zero8
        for p in range(8):
            zs3[t, p * PITCH3:p * PITCH3 + 8, :] = zero8
            zs3[t, p * PITCH3 + 24:p * PITCH3 + 32, :] = zero8
        for p in range(5, 8):
            for r in (8, 16):
                zs3[t, p * PITCH3 + r:p * PITCH3 + r + 8, :] = zero8

    flag = {key: jnp.where(value, 1.0, 0.0).astype(F32) for key, value in has.items()}
    zlo, zhi = flag["gz", -1], flag["gz", 1]
    ylo, yhi = flag["gy", -1], flag["gy", 1]
    lane = lax.broadcasted_iota(jnp.int32, (8, LANES), 1)
    sub = lax.broadcasted_iota(jnp.int32, (8, LANES), 0)
    xflag = jnp.where(lane < 64, flag["gx", 1], flag["gx", -1])

    def level_one_tiles(b):
        cols = slice(256 * b, 256 * b + 256)
        for i in range(-1, 9):
            plane = reduce_planes(lambda s: v[s, :, cols], 0, 15, i)
            row = (i + 1) * PITCH1 + 8
            for h in range(2):
                zs1[2 * b + h, row:row + 64, :] = plane[:, 128 * h:128 * h + 128]
        for c in (2 * b, 2 * b + 1):
            for i in range(-1, 9):
                base = (i + 1) * PITCH1 + 8
                plane = weighted({k: zs1[c, pl.ds(base + k - 2, 32, stride=2), :] for k in range(5)})
                if i == -1:
                    as1[c, 256:288, :] = plane * zlo
                elif i == 8:
                    as1[c, 288:320, :] = plane * zhi
                else:
                    as1[c, 32 * i:32 * i + 32, :] = plane

            def column(y, p, size):
                return zs1[c, pl.ds(p * PITCH1 + 8 + y, size, stride=PITCH1), :]

            as1[c, 320:328, :] = column(0, 1, 8) * ylo
            as1[c, 336:344, :] = weighted({0: column(62, 1, 8), 1: column(63, 1, 8)}) * yhi
            for s, p, zflag in ((0, 0, zlo), (1, 9, zhi)):
                first = p * PITCH1 + 8
                as1[c, 328 + s:329 + s, :] = zs1[c, first:first + 1, :] * (ylo * zflag)
                as1[c, 344 + s:345 + s, :] = weighted(
                    {0: zs1[c, first + 62:first + 63, :], 1: zs1[c, first + 63:first + 64, :]}
                ) * (yhi * zflag)
        for r in range(0, ROWS1, 176):
            rows = slice(r, r + 176)
            block = jnp.concatenate([as1[2 * b, rows, :], as1[2 * b + 1, rows, :]], axis=1)
            p1[b, rows, :] = product(block, band[...])

    def combine(parts, result, tiles, rows, mask):
        size = 16
        low = lax.broadcasted_iota(jnp.int32, (size, LANES), 1) < 64
        wide = None if mask is None else jnp.broadcast_to(mask[0:1], (size, LANES))
        total = tiles + 1
        for r in range(0, rows, size):
            over = [parts(t, r, size, 1) for t in range(total)]
            for t in range(total):
                before, after = over[(t - 1) % total], over[(t + 1) % total]
                if before is None:
                    spill = jnp.where(low, 0.0, after)
                elif after is None:
                    spill = jnp.where(low, before, 0.0)
                else:
                    spill = jnp.where(low, before, after)
                main = parts(t, r, size, 0)
                value = spill if main is None else main + spill
                if t == tiles and wide is not None:
                    value = value * wide
                result[t, r:r + size, :] = value

    for b in order:
        loads[b].wait()
        level_one_tiles(b)

    def parts1(t, r, size, half):
        return None if t == 4 else p1[t, r:r + size, 128 * half:128 * half + 128]

    combine(parts1, l1, 4, ROWS1, xflag)

    zflag2 = jnp.where(sub == 0, zlo, jnp.where(sub < 5, 1.0, zhi))
    plane_row1 = lambda s: 256 if s == -1 else (288 if s == 8 else 32 * s)
    plane_row2 = lambda s: 64 if s == -1 else (80 + 16 * (s - 4) if s >= 4 else 16 * s)
    plane_row3 = lambda s: 16 if s == -1 else (24 + 8 * (s - 2) if s >= 2 else 8 * s)
    zscale2 = lambda i: zlo if i == -1 else (zhi if i >= 4 else None)
    for t in range(5):
        for e, first in ((0, 320), (1, 336)):
            ye1[t, e, 8:16, :] = l1[t, first:first + 8, :]
            ye1[t, e, 7:8, :] = l1[t, first + 8:first + 9, :]
            ye1[t, e, 16:17, :] = l1[t, first + 9:first + 10, :]
        for i in range(-1, 6):
            plane = reduce_planes(lambda s: l1[t, plane_row1(s):plane_row1(s) + 32, :], -1, 8, i)
            if zscale2(i) is not None:
                plane = plane * zscale2(i)
            row = (i + 1) * PITCH2 + 8
            zs2[t, row:row + 32, :] = plane
        for e, y in ((0, -1), (1, 32)):
            block = weighted({k: ye1[t, e, pl.ds(4 + k, 8, stride=2), :] for k in range(5)})
            zs2[t, pl.ds(8 + y, 8, stride=PITCH2), :] = block * zflag2
        for i in range(-1, 6):
            base = (i + 1) * PITCH2 + 8
            row = plane_row2(i)
            as2[t, row:row + 16, :] = weighted(
                {k: zs2[t, pl.ds(base + k - 2, 16, stride=2), :] for k in range(5)}
            )

        def column2(y):
            return zs2[t, pl.ds(8 + y, 8, stride=PITCH2), :]

        as2[t, 112:120, :] = weighted({3: column2(-1), 4: column2(0)}) * ylo
        as2[t, 120:128, :] = weighted({0: column2(30), 1: column2(31), 2: column2(32)}) * yhi
        as2[t, 128:136, :] = column2(32) * yhi
    for b in range(2):
        block = jnp.concatenate([as2[2 * b], as2[2 * b + 1]], axis=1)
        p2[b] = product(block, band[...])
    p2[2] = product(as2[4], edge[...])

    def parts2(t, r, size, half):
        return p2[t, r:r + size, 128 * half:128 * half + 128]

    combine(parts2, l2, 2, ROWS2, xflag)

    for t in range(3):
        for e, first in ((0, 112), (1, 120), (2, 128)):
            ye2[t, e, 7:15, :] = l2[t, first:first + 8, :]
        for i in range(-1, 4):
            row = (i + 1) * PITCH3 + 8
            zs3[t, row:row + 16, :] = reduce_planes(
                lambda s: l2[t, plane_row2(s):plane_row2(s) + 16, :], -1, 5, i
            )
        for e, y in ((0, -1), (1, 16), (2, 17)):
            block = weighted({k: ye2[t, e, pl.ds(4 + k, 8, stride=2), :] for k in range(5)})
            zs3[t, pl.ds(8 + y, 8, stride=PITCH3), :] = block
        for i in range(-1, 4):
            base = (i + 1) * PITCH3 + 8
            row = plane_row3(i)
            as3[t, row:row + 8, :] = weighted(
                {k: zs3[t, pl.ds(base + k - 2, 8, stride=2), :] for k in range(5)}
            )

        def column3(y):
            return zs3[t, pl.ds(8 + y, 8, stride=PITCH3), :]

        as3[t, 40:48, :] = weighted({3: column3(-1), 4: column3(0)})
        as3[t, 48:56, :] = weighted({k: column3(14 + k) for k in range(4)})
        as3[t, 56:64, :] = weighted({0: column3(16), 1: column3(17)})
    p3[0] = product(jnp.concatenate([as3[0], as3[1]], axis=1), band[...])
    p3[1] = product(as3[2], edge[...])

    def parts3(t, r, size, half):
        return p3[t, r:r + size, 128 * half:128 * half + 128]

    combine(parts3, l3, 1, ROWS3, None)

    main_groups = [(l1, 4, 8 * g) for g in range(32)] + [(l2, 2, 8 * g) for g in range(8)] + [(l3, 1, 8 * g) for g in range(2)]
    side_groups = [(l1, 4, 256 + 8 * g) for g in range(12)] + [(l2, 2, 64 + 8 * g) for g in range(9)] + [(l3, 1, 16 + 8 * g) for g in range(6)]
    side_index = {("1", 256 + 8 * g): g for g in range(12)}
    side_index.update({("2", 64 + 8 * g): 12 + g for g in range(9)})
    side_index.update({("3", 16 + 8 * g): 21 + g for g in range(6)})

    def pack(groups):
        total = None
        for g, (ref, t, row) in enumerate(groups):
            piece = ref[t, row:row + 8, :]
            piece = piece if g == 0 else pltpu.roll(piece, 3 * g, 1)
            total = piece if total is None else total + piece
        return total

    xm[...] = pack(main_groups)
    xs[...] = pack(side_groups)

    def transfers(d):
        dz, dy, dx = d
        if dx:
            if dz == 0 and dy == 0:
                return [(xm, rxm.at[0 if dx == 1 else 1])]
            return [(xs, rxs.at[0 if dx == 1 else 1, SIDE[dz, dy]])]
        if dy == 0:
            if dz == 1:
                return [
                    (l1.at[pl.ds(0, 4), pl.ds(288, 32), :], rz1.at[0]),
                    (l2.at[pl.ds(0, 2), pl.ds(80, 32), :], rz2u),
                    (l3.at[pl.ds(0, 1), pl.ds(24, 16), :], rz3u),
                ]
            return [
                (l1.at[pl.ds(0, 4), pl.ds(256, 32), :], rz1.at[1]),
                (l2.at[pl.ds(0, 2), pl.ds(64, 16), :], rz2d),
                (l3.at[pl.ds(0, 1), pl.ds(16, 8), :], rz3d),
            ]
        side = SIDE[dz, dy]
        first2, first3, size = (120, 48, 16) if dy == 1 else (112, 40, 8)
        first1 = (336 if dy == 1 else 320) + (8 if dz else 0)
        return [
            (l1.at[pl.ds(0, 4), pl.ds(first1, 8), :], ry1.at[side]),
            (l2.at[pl.ds(0, 2), pl.ds(first2, size), :], ry2.at[side, :, pl.ds(0, size), :]),
            (l3.at[pl.ds(0, 1), pl.ds(first3, size), :], ry3.at[side, :, pl.ds(0, size), :]),
        ]

    def copies(d):
        return [
            pltpu.make_async_remote_copy(
                src_ref=source,
                dst_ref=target,
                send_sem=send_sem.at[SLOT[d], i],
                recv_sem=recv_sem.at[SLOT[d], i],
                device_id=device(d),
                device_id_type=MESH,
            )
            for i, (source, target) in enumerate(transfers(d))
        ]

    near = 1
    for axis in me:
        near = near * (1 + has[axis, 1].astype(jnp.int32) + has[axis, -1].astype(jnp.int32))
    pl.semaphore_wait(barrier, near - 1)

    for d in DIRECTIONS:
        @pl.when(exists(d))
        def _():
            for copy in copies(d):
                copy.start()

    def add_side(dz, dy, get, tiles):
        for level, ref in (("1", l1), ("2", l2), ("3", l3)):
            for t in tiles(level):
                height = {"1": 32, "2": 16, "3": 8}[level]
                depth = {"1": 8, "2": 4, "3": 2}[level]
                if dy == 0:
                    if dz == 1:
                        first = {"1": 288, "2": 80, "3": 24}[level]
                        size = height if level == "1" else 2 * height
                        to = 0
                    else:
                        first = {"1": 256, "2": 64, "3": 16}[level]
                        size = height
                        to = (depth - 1) * height
                    for r in range(0, size, 8):
                        rows = slice(to + r, to + r + 8)
                        ref[t, rows, :] = ref[t, rows, :] + get(level, first + r, t)
                    continue
                if dy == 1:
                    blocks = {"1": ((336, 0),), "2": ((120, 0), (128, 1)), "3": ((48, 0), (56, 1))}[level]
                else:
                    blocks = {"1": ((320, 31),), "2": ((112, 15),), "3": ((40, 7),)}[level]
                for first, y in blocks:
                    if dz == 0:
                        value = get(level, first, t)
                        value = value if level == "1" else value[1:1 + depth]
                        rows = pl.ds(y, depth, stride=height)
                        ref[t, rows, :] = ref[t, rows, :] + value
                        continue
                    if level == "1":
                        value = get(level, first + 8, t)
                        pairs = ((1, 0),) if dz == 1 else ((0, depth - 1),)
                    else:
                        value = get(level, first, t)
                        pairs = ((depth + 1, 0), (depth + 2, 1)) if dz == 1 else ((0, depth - 1),)
                    for s, z in pairs:
                        row = slice(z * height + y, z * height + y + 1)
                        ref[t, row, :] = ref[t, row, :] + value[s:s + 1]

    def arrive(d):
        dz, dy, dx = d
        for copy in copies(d):
            copy.wait_recv()
        if dx == 0:
            def get(level, row, t):
                if dy == 0:
                    box = {
                        ("1", 1): (rz1.at[0], 288), ("2", 1): (rz2u, 80), ("3", 1): (rz3u, 24),
                        ("1", -1): (rz1.at[1], 256), ("2", -1): (rz2d, 64), ("3", -1): (rz3d, 16),
                    }[level, dz]
                    return box[0][t, row - box[1]:row - box[1] + 8, :]
                first2, first3 = (120, 48) if dy == 1 else (112, 40)
                side = SIDE[dz, dy]
                if level == "1":
                    return ry1[side, t, :, :]
                if level == "2":
                    return ry2[side, t, row - first2:row - first2 + 8, :]
                return ry3[side, t, row - first3:row - first3 + 8, :]

            add_side(dz, dy, get, lambda level: range({"1": 4, "2": 2, "3": 1}[level]))
            return
        keep = lane < 2 if dx == 1 else lane == 127
        column = 0 if dx == 1 else 1

        def spread(value, g):
            moved = value if g == 0 else pltpu.roll(value, LANES - 3 * g, 1)
            return jnp.where(keep, moved, 0.0)

        if dz == 0 and dy == 0:
            value = rxm[column]
            for g, (ref, last, row) in enumerate(main_groups):
                t = 0 if dx == 1 else last - 1
                ref[t, row:row + 8, :] = ref[t, row:row + 8, :] + spread(value, g)
            return
        value = rxs[column, SIDE[dz, dy]]
        add_side(
            dz, dy,
            lambda level, row, t: spread(value, side_index[level, row]),
            lambda level: (0 if dx == 1 else {"1": 3, "2": 1, "3": 0}[level],),
        )

    incoming = sorted(DIRECTIONS, key=lambda d: (d[2] != 0, sum(map(abs, d)), -abs(d[1])))
    for d in incoming:
        @pl.when(exists(tuple(-s for s in d)))
        def _():
            arrive(d)

    for z in range(8):
        for t in range(4):
            out1[z, :, LANES * t:LANES * t + LANES] = l1[t, 32 * z:32 * z + 32, :]
    for z in range(4):
        for t in range(2):
            out2[z, :, LANES * t:LANES * t + LANES] = l2[t, 16 * z:16 * z + 16, :]
    for z in range(2):
        out3[z, :, :] = l3[0, 8 * z:8 * z + 8, :]

    for d in DIRECTIONS:
        @pl.when(exists(d))
        def _():
            for copy in copies(d):
                copy.wait_send()


def on_device(counts, volume):
    vmem = lambda *shape: pltpu.VMEM(shape, F32)
    return pl.pallas_call(
        functools.partial(pyramid, counts),
        out_shape=(
            jax.ShapeDtypeStruct((8, 32, 512), F32),
            jax.ShapeDtypeStruct((4, 16, 256), F32),
            jax.ShapeDtypeStruct((2, 8, 128), F32),
        ),
        in_specs=[pl.BlockSpec(memory_space=pl.ANY)],
        out_specs=[pl.BlockSpec(memory_space=pltpu.VMEM)] * 3,
        scratch_shapes=[
            vmem(16, 64, 1024),
            vmem(8, 10 * PITCH1 + 8, LANES), vmem(8, ROWS1, LANES), vmem(4, ROWS1, 256), vmem(5, ROWS1, LANES),
            vmem(5, 2, 24, LANES), vmem(5, 8 * PITCH2, LANES), vmem(5, ROWS2, LANES), vmem(3, ROWS2, 256),
            vmem(3, ROWS2, LANES),
            vmem(3, 3, 24, LANES), vmem(3, 8 * PITCH3, LANES), vmem(3, ROWS3, LANES), vmem(2, ROWS3, 256),
            vmem(2, ROWS3, LANES),
            pltpu.VMEM((256, 256), BF16), pltpu.VMEM((128, 256), BF16),
            vmem(8, LANES), vmem(8, LANES),
            vmem(2, 4, 32, LANES), vmem(2, 32, LANES), vmem(2, 16, LANES), vmem(1, 16, LANES), vmem(1, 8, LANES),
            vmem(8, 4, 8, LANES), vmem(8, 2, 16, LANES), vmem(8, 1, 16, LANES),
            vmem(2, 8, LANES), vmem(2, 8, 8, LANES),
            pltpu.SemaphoreType.DMA((4,)),
            pltpu.SemaphoreType.DMA((26, 3)),
            pltpu.SemaphoreType.DMA((26, 3)),
        ],
        compiler_params=pltpu.CompilerParams(
            collective_id=0, has_side_effects=True, vmem_limit_bytes=40 * 1024 * 1024
        ),
        name="pyramid",
    )(volume)


def solution(mesh):
    spec = P("gz", "gy", "gx")
    return jax.shard_map(
        functools.partial(on_device, dict(mesh.shape)),
        mesh=mesh,
        in_specs=(spec,),
        out_specs=(spec, spec, spec),
        check_vma=False,
    )
```

time: 222 us -> 22.5 us (0.10)
  the two profiles are of different devices: /device:TPU:66 before, /device:TPU:75 now
where the time goes in v1:
time: 22.5 us; the launch traced here: 22.4 us
  Pallas kernels  17.5 us (78%)
  local copies, waits for them, and re-layouts  4.2 us (19%)
  between operations  0.65 us (3%)
    pallas_call x1, Pallas kernels, on_device(): pl.pallas_call(functools.partial(pyramid, counts), out_shape=(jax.ShapeDt...  17.5 us
    unnamed x5, local copies, waits for them, and re-layouts  4.2 us

profile of v1, /device:TPU:75, one launch (start us, length us, event | category | flops | bytes accessed | tf_op | source)
XLA Modules:
  0.0 22.4 jit_solution(13569133801541599068)
XLA Ops:
  0.6 0.0 copy-start
  0.6 2.2 %copy-done = f32[16,64,1024]{2,1,0:T(8,128)S(1)} copy-done((f32[16,64,1024]{2,1,0:T(8,128)S(1)}, f32[16,64,1024]{2,1,0:T(8,128)}, u32[]{:S(2)}) %copy-start) | copy-done | bytes 4194328
  2.8 17.5 %pyramid.1 = (f32[8,32,512]{2,1,0:T(8,128)S(1)}, f32[4,16,256]{2,1,0:T(8,128)S(1)}, f32[2,8,128]{2,1,0:T(8,128)S(1)}) custom-call(f32[16,64,1024]{2,1,0:T(8,128)S(1)} %copy-done), custom_call_target="tpu_custom_call" | custom-call | tf_op jit(solution)/shard_map/pyramid/pallas_call | solution.py:463
  20.4 0.8 %copy.7 = f32[8,32,512]{2,1,0:T(8,128)} copy(f32[8,32,512]{2,1,0:T(8,128)S(1)} %get-tuple-element.6) | data formatting | bytes 1048576
  21.2 0.6 %copy.8 = f32[4,16,256]{2,1,0:T(8,128)} copy(f32[4,16,256]{2,1,0:T(8,128)S(1)} %get-tuple-element.7) | data formatting | bytes 131072
  21.8 0.6 %copy.9 = f32[2,8,128]{2,1,0:T(8,128)} copy(f32[2,8,128]{2,1,0:T(8,128)S(1)} %get-tuple-element.8) | data formatting | bytes 16384
Async XLA Ops:
  0.6 2.2 %copy-start = (f32[16,64,1024]{2,1,0:T(8,128)S(1)}, f32[16,64,1024]{2,1,0:T(8,128)}, u32[]{:S(2)}) copy-start(f32[16,64,1024]{2,1,0:T(8,128)} %vol.1) | copy-start | bytes 12582916

commit v2 on v1

--- a/solution.py
+++ b/solution.py
@@ -17,14 +17,18 @@
 PITCH1, PITCH2, PITCH3 = 72, 48, 32
 DIRECTIONS = [
     (dz, dy, dx)
-    for dx in (1, -1, 0)
+    for dx in (-1, 1, 0)
     for dz in (1, -1, 0)
-    for dy in (1, -1, 0)
+    for dy in (-1, 1, 0)
     if (dz, dy, dx) != (0, 0, 0)
 ]
 SLOT = {d: i for i, d in enumerate(DIRECTIONS)}
 SIDES = [(dz, dy) for dz in (1, -1, 0) for dy in (1, -1, 0) if (dz, dy) != (0, 0)]
 SIDE = {d: i for i, d in enumerate(SIDES)}
+UPPER = [d for d in DIRECTIONS if (d[2], d[1], d[0]) > (0, 0, 0)]
+LOWER = [d for d in DIRECTIONS if (d[2], d[1], d[0]) < (0, 0, 0)]
+FACES = [(1, 0, 0), (-1, 0, 0), (0, 1, 0), (0, -1, 0)]
+CORNER = {(1, 1): 0, (1, -1): 1, (-1, 1): 2, (-1, -1): 3}
 
 
 def weighted(pieces):
@@ -82,8 +86,8 @@
 
 
 def pyramid(counts, vol, out1, out2, out3, v, zs1, as1, p1, l1, ye1, zs2, as2, p2, l2, ye2, zs3, as3, p3, l3,
-            band, edge, xm, xs, rz1, rz2u, rz2d, rz3u, rz3d, ry1, ry2, ry3, rxm, rxs,
-            load_sem, send_sem, recv_sem):
+            band, edge, xp, yf, q, rz1, rz2u, rz2d, rz3u, rz3d, ry1, ryf, rq, rx, rr,
+            load_sem, send_sem, recv_sem, ready):
     me = {axis: lax.axis_index(axis) for axis in ("gz", "gy", "gx")}
     has = {(axis, 1): me[axis] < counts[axis] - 1 for axis in me}
     has.update({(axis, -1): me[axis] > 0 for axis in me})
@@ -97,6 +101,27 @@
 
     def device(d):
         return {axis: me[axis] + step for axis, step in zip(("gz", "gy", "gx"), d) if step}
+
+    def blank(d):
+        dz, dy, dx = d
+        zeros = jnp.zeros((8, LANES), F32)
+        if dx:
+            column = 0 if dx == 1 else 1
+            target = rr.at[SIDE[dz, dy], column] if dz or dy else rx.at[column]
+            target[...] = zeros
+            return
+        side = 0 if dy == 1 else 1
+        if dz and dy:
+            targets = [rq.at[CORNER[dz, dy]]]
+        elif dy:
+            targets = [ry1.at[side, t] for t in range(4)] + [ryf.at[side, t] for t in range(3)]
+        elif dz == 1:
+            targets = [rz1.at[0, t] for t in range(4)] + [rz2u.at[t] for t in range(2)] + [rz3u.at[0]]
+        else:
+            targets = [rz1.at[1, t] for t in range(4)] + [rz2d.at[t] for t in range(2)] + [rz3d.at[0]]
+        for target in targets:
+            for r in range(0, target.shape[0], 8):
+                target[r:r + 8, :] = zeros
 
     order = (0, 3, 1, 2)
     loads = [
@@ -109,10 +134,27 @@
         loads[b].start()
 
     barrier = pltpu.get_barrier_semaphore()
-    for d in DIRECTIONS:
-        @pl.when(exists(d))
-        def _():
-            pl.semaphore_signal(barrier, inc=1, device_id=device(d), device_id_type=MESH)
+    interior = functools.reduce(lambda x, y: x & y, has.values())
+
+    def signal(semaphore, d):
+        pl.semaphore_signal(semaphore, inc=1, device_id=device(d), device_id_type=MESH)
+
+    @pl.when(interior)
+    def _():
+        for d in UPPER:
+            signal(barrier, d)
+
+    @pl.when(jnp.logical_not(interior))
+    def _():
+        for d in UPPER:
+            @pl.when(exists(d))
+            def _():
+                signal(barrier, d)
+
+        for d in DIRECTIONS:
+            @pl.when(jnp.logical_not(exists(tuple(-k for k in d))))
+            def _():
+                blank(d)
 
     build_weights(band, edge)
     zero8 = jnp.zeros((8, LANES), F32)
@@ -121,6 +163,12 @@
             zs1[c, p * PITCH1:p * PITCH1 + 8, :] = zero8
         as1[c, 328:336, :] = zero8
         as1[c, 344:352, :] = zero8
+    for c in range(4):
+        q[c, 0:8, :] = zero8
+        q[c, 8:16, :] = zero8
+    for side in range(2):
+        for t in range(3):
+            yf[side, t] = zero8
     for t in range(5):
         for e in range(2):
             for r in range(0, 24, 8):
@@ -149,13 +197,75 @@
     sub = lax.broadcasted_iota(jnp.int32, (8, LANES), 0)
     xflag = jnp.where(lane < 64, flag["gx", 1], flag["gx", -1])
 
+    def transfers(d):
+        dz, dy, dx = d
+        if dx:
+            column = 0 if dx == 1 else 1
+            if dz == 0 and dy == 0:
+                return {2: (xp.at[0], rx.at[column])}
+            return {2: (xp.at[1], rr.at[SIDE[dz, dy], column])}
+        if dy == 0:
+            if dz == 1:
+                return {
+                    0: (l1.at[pl.ds(0, 4), pl.ds(288, 32), :], rz1.at[0]),
+                    1: (l2.at[pl.ds(0, 2), pl.ds(80, 32), :], rz2u),
+                    2: (l3.at[pl.ds(0, 1), pl.ds(24, 16), :], rz3u),
+                }
+            return {
+                0: (l1.at[pl.ds(0, 4), pl.ds(256, 32), :], rz1.at[1]),
+                1: (l2.at[pl.ds(0, 2), pl.ds(64, 16), :], rz2d),
+                2: (l3.at[pl.ds(0, 1), pl.ds(16, 8), :], rz3d),
+            }
+        if dz == 0:
+            side = 0 if dy == 1 else 1
+            return {
+                0: (l1.at[pl.ds(0, 4), pl.ds(336 if dy == 1 else 320, 8), :], ry1.at[side]),
+                2: (yf.at[side], ryf.at[side]),
+            }
+        corner = CORNER[dz, dy]
+        return {2: (q.at[corner], rq.at[corner])}
+
+    def copies(d, stages=(0, 1, 2)):
+        return [
+            pltpu.make_async_remote_copy(
+                src_ref=pair[0],
+                dst_ref=pair[1],
+                send_sem=send_sem.at[SLOT[d], i],
+                recv_sem=recv_sem.at[SLOT[d], i],
+                device_id=device(d),
+                device_id_type=MESH,
+            )
+            for i, pair in transfers(d).items()
+            if i in stages
+        ]
+
+    def for_neighbours(act, stages=(0, 1, 2), back=False, only=None):
+        chosen = [d for d in (only or DIRECTIONS) if any(i in stages for i in transfers(d))]
+
+        @pl.when(interior)
+        def _():
+            for d in chosen:
+                for copy in copies(d, stages):
+                    act(copy)
+
+        @pl.when(jnp.logical_not(interior))
+        def _():
+            for d in chosen:
+                @pl.when(exists(tuple(-k for k in d) if back else d))
+                def _():
+                    for copy in copies(d, stages):
+                        act(copy)
+
+    start, received, sent = (lambda c: c.start()), (lambda c: c.wait_recv()), (lambda c: c.wait_send())
+
     def level_one_tiles(b):
-        cols = slice(256 * b, 256 * b + 256)
-        for i in range(-1, 9):
-            plane = reduce_planes(lambda s: v[s, :, cols], 0, 15, i)
-            row = (i + 1) * PITCH1 + 8
-            for h in range(2):
-                zs1[2 * b + h, row:row + 64, :] = plane[:, 128 * h:128 * h + 128]
+        for r in range(0, 64, 8):
+            planes = [v[s, r:r + 8, 256 * b:256 * b + 256] for s in range(16)]
+            for i in range(-1, 9):
+                plane = reduce_planes(lambda s: planes[s], 0, 15, i)
+                row = (i + 1) * PITCH1 + 8 + r
+                for h in range(2):
+                    zs1[2 * b + h, row:row + 8, :] = plane[:, 128 * h:128 * h + 128]
         for c in (2 * b, 2 * b + 1):
             for i in range(-1, 9):
                 base = (i + 1) * PITCH1 + 8
@@ -212,7 +322,35 @@
         return None if t == 4 else p1[t, r:r + size, 128 * half:128 * half + 128]
 
     combine(parts1, l1, 4, ROWS1, xflag)
-
+    one = {key: value.astype(jnp.int32) for key, value in has.items()}
+    across_z = 1 + one["gz", 1] + one["gz", -1]
+    across = across_z * (1 + one["gy", 1] + one["gy", -1])
+    near_lower, near_upper = (one["gy", k] * across_z + one["gz", k] for k in (-1, 1))
+    far_lower, far_upper = (one["gx", k] * across for k in (-1, 1))
+
+    def wait_for(semaphore, number):
+        @pl.when(number > 0)
+        def _():
+            pl.semaphore_wait(semaphore, number)
+
+    wait_for(barrier, near_lower + far_lower)
+
+    def answer(d):
+        signal(ready.at[1 if d[2] else 0], d)
+
+    @pl.when(interior)
+    def _():
+        for d in LOWER:
+            answer(d)
+
+    @pl.when(jnp.logical_not(interior))
+    def _():
+        for d in LOWER:
+            @pl.when(exists(d))
+            def _():
+                answer(d)
+
+    for_neighbours(start, (0,), only=LOWER)
     zflag2 = jnp.where(sub == 0, zlo, jnp.where(sub < 5, 1.0, zhi))
     plane_row1 = lambda s: 256 if s == -1 else (288 if s == 8 else 32 * s)
     plane_row2 = lambda s: 64 if s == -1 else (80 + 16 * (s - 4) if s >= 4 else 16 * s)
@@ -254,6 +392,7 @@
         return p2[t, r:r + size, 128 * half:128 * half + 128]
 
     combine(parts2, l2, 2, ROWS2, xflag)
+    for_neighbours(start, (1,), only=LOWER)
 
     for t in range(3):
         for e, first in ((0, 112), (1, 120), (2, 128)):
@@ -289,9 +428,6 @@
 
     main_groups = [(l1, 4, 8 * g) for g in range(32)] + [(l2, 2, 8 * g) for g in range(8)] + [(l3, 1, 8 * g) for g in range(2)]
     side_groups = [(l1, 4, 256 + 8 * g) for g in range(12)] + [(l2, 2, 64 + 8 * g) for g in range(9)] + [(l3, 1, 16 + 8 * g) for g in range(6)]
-    side_index = {("1", 256 + 8 * g): g for g in range(12)}
-    side_index.update({("2", 64 + 8 * g): 12 + g for g in range(9)})
-    side_index.update({("3", 16 + 8 * g): 21 + g for g in range(6)})
 
     def pack(groups):
         total = None
@@ -301,146 +437,142 @@
             total = piece if total is None else total + piece
         return total
 
-    xm[...] = pack(main_groups)
-    xs[...] = pack(side_groups)
-
-    def transfers(d):
-        dz, dy, dx = d
-        if dx:
-            if dz == 0 and dy == 0:
-                return [(xm, rxm.at[0 if dx == 1 else 1])]
-            return [(xs, rxs.at[0 if dx == 1 else 1, SIDE[dz, dy]])]
-        if dy == 0:
-            if dz == 1:
-                return [
-                    (l1.at[pl.ds(0, 4), pl.ds(288, 32), :], rz1.at[0]),
-                    (l2.at[pl.ds(0, 2), pl.ds(80, 32), :], rz2u),
-                    (l3.at[pl.ds(0, 1), pl.ds(24, 16), :], rz3u),
-                ]
-            return [
-                (l1.at[pl.ds(0, 4), pl.ds(256, 32), :], rz1.at[1]),
-                (l2.at[pl.ds(0, 2), pl.ds(64, 16), :], rz2d),
-                (l3.at[pl.ds(0, 1), pl.ds(16, 8), :], rz3d),
-            ]
-        side = SIDE[dz, dy]
-        first2, first3, size = (120, 48, 16) if dy == 1 else (112, 40, 8)
-        first1 = (336 if dy == 1 else 320) + (8 if dz else 0)
-        return [
-            (l1.at[pl.ds(0, 4), pl.ds(first1, 8), :], ry1.at[side]),
-            (l2.at[pl.ds(0, 2), pl.ds(first2, size), :], ry2.at[side, :, pl.ds(0, size), :]),
-            (l3.at[pl.ds(0, 1), pl.ds(first3, size), :], ry3.at[side, :, pl.ds(0, size), :]),
-        ]
-
-    def copies(d):
-        return [
-            pltpu.make_async_remote_copy(
-                src_ref=source,
-                dst_ref=target,
-                send_sem=send_sem.at[SLOT[d], i],
-                recv_sem=recv_sem.at[SLOT[d], i],
-                device_id=device(d),
-                device_id_type=MESH,
-            )
-            for i, (source, target) in enumerate(transfers(d))
-        ]
-
-    near = 1
-    for axis in me:
-        near = near * (1 + has[axis, 1].astype(jnp.int32) + has[axis, -1].astype(jnp.int32))
-    pl.semaphore_wait(barrier, near - 1)
-
-    for d in DIRECTIONS:
-        @pl.when(exists(d))
-        def _():
-            for copy in copies(d):
-                copy.start()
-
-    def add_side(dz, dy, get, tiles):
-        for level, ref in (("1", l1), ("2", l2), ("3", l3)):
-            for t in tiles(level):
-                height = {"1": 32, "2": 16, "3": 8}[level]
-                depth = {"1": 8, "2": 4, "3": 2}[level]
-                if dy == 0:
-                    if dz == 1:
-                        first = {"1": 288, "2": 80, "3": 24}[level]
-                        size = height if level == "1" else 2 * height
-                        to = 0
+    for side, blocks2, blocks3 in ((0, (120, 128), (48, 56)), (1, (112,), (40,))):
+        for t in range(2):
+            for j, row in enumerate(blocks2):
+                yf[side, t, 4 * j:4 * j + 4, :] = l2[t, row + 1:row + 5, :]
+        for j, row in enumerate(blocks3):
+            yf[side, 2, 2 * j:2 * j + 2, :] = l3[0, row + 1:row + 3, :]
+        for dz in (1, -1):
+            corner = CORNER[dz, 1 - 2 * side]
+            row1 = (344 if side == 0 else 328) + (1 if dz == 1 else 0)
+            first2, first3, size = (5, 3, 2) if dz == 1 else (0, 0, 1)
+            for t in range(4):
+                q[corner, t:t + 1, :] = l1[t, row1:row1 + 1, :]
+            for t in range(2):
+                for j, row in enumerate(blocks2):
+                    to = 8 + 4 * t + 2 * j
+                    q[corner, to:to + size, :] = l2[t, row + first2:row + first2 + size, :]
+            for j, row in enumerate(blocks3):
+                q[corner, 4 + 2 * j:4 + 2 * j + size, :] = l3[0, row + first3:row + first3 + size, :]
+
+    xp[0] = pack(main_groups)
+    xp[1] = pack(side_groups)
+
+    for_neighbours(start, (2,), only=LOWER)
+    wait_for(ready.at[0], near_upper)
+    for_neighbours(start, only=[d for d in UPPER if d[2] == 0])
+    wait_for(ready.at[1], far_upper)
+    for_neighbours(start, only=[d for d in UPPER if d[2]])
+
+    heights, depths = (32, 16, 8), (8, 4, 2)
+    levels = (l1, l2, l3)
+
+    def add(level, t, rows, value):
+        ref = levels[level]
+        ref[t, rows, :] = ref[t, rows, :] + value
+
+    def add_y(dy, level, t, get):
+        height, depth = heights[level], depths[level]
+        for j in range(2 if dy == 1 and level else 1):
+            add(level, t, pl.ds(j if dy == 1 else height - 1, depth, stride=height), get(j))
+
+    def add_z(dz, level, t, get):
+        height, depth = heights[level], depths[level]
+        planes = 2 if dz == 1 and level else 1
+        to = 0 if dz == 1 else (depth - 1) * height
+        for r in range(0, planes * height, 8):
+            add(level, t, slice(to + r, to + r + 8), get(r))
+
+    def add_corner(dz, dy, level, t, get):
+        height, depth = heights[level], depths[level]
+        planes = 2 if dz == 1 and level else 1
+        for j in range(2 if dy == 1 and level else 1):
+            value = get(j)
+            for p in range(planes):
+                row = (p if dz == 1 else depth - 1) * height + (j if dy == 1 else height - 1)
+                add(level, t, slice(row, row + 1), value[p:p + 1])
+
+    for_neighbours(received, (0, 1, 2), back=True, only=[d for d in DIRECTIONS if d[1] and not d[2]])
+    for dy in (1, -1):
+        side = 0 if dy == 1 else 1
+        for t in range(4):
+            add_y(dy, 0, t, lambda j: ry1[side, t])
+        for t in range(2):
+            add_y(dy, 1, t, lambda j: ryf[side, t, 4 * j:4 * j + 4, :])
+        add_y(dy, 2, 0, lambda j: ryf[side, 2, 2 * j:2 * j + 2, :])
+        for dz in (1, -1):
+            c = CORNER[dz, dy]
+            for t in range(4):
+                add_corner(dz, dy, 0, t, lambda j: rq[c, t:t + 1, :])
+            for t in range(2):
+                add_corner(dz, dy, 1, t, lambda j: rq[c, 8 + 4 * t + 2 * j:10 + 4 * t + 2 * j, :])
+            add_corner(dz, dy, 2, 0, lambda j: rq[c, 4 + 2 * j:6 + 2 * j, :])
+    for_neighbours(received, (0, 1, 2), back=True, only=FACES[:2])
+    for t in range(4):
+        add_z(1, 0, t, lambda r: rz1[0, t, r:r + 8, :])
+        add_z(-1, 0, t, lambda r: rz1[1, t, r:r + 8, :])
+    for t in range(2):
+        add_z(1, 1, t, lambda r: rz2u[t, r:r + 8, :])
+        add_z(-1, 1, t, lambda r: rz2d[t, r:r + 8, :])
+    add_z(1, 2, 0, lambda r: rz3u[0, r:r + 8, :])
+    add_z(-1, 2, 0, lambda r: rz3d[0, r:r + 8, :])
+    for_neighbours(received, back=True, only=[d for d in DIRECTIONS if d[2]])
+    third = lax.rem(lane, 3)
+    low_lanes, high_lane = lane < 2, lane == 127
+
+    def both(low_side, high_side):
+        return jnp.where((third == 2) | high_lane, high_side, low_side)
+
+    def spread(value, g):
+        moved = value if g == 0 else pltpu.roll(value, LANES - 3 * g, 1)
+        return jnp.where(low_lanes, moved, 0.0), jnp.where(high_lane, moved, 0.0)
+
+    def add_columns(level, pairs):
+        last = (3, 1, 0)[level]
+        for rows, (low_value, high_value) in pairs:
+            if last == 0:
+                add(level, 0, rows, low_value + high_value)
+            else:
+                add(level, 0, rows, low_value)
+                add(level, last, rows, high_value)
+
+    value = both(rx[0], rx[1])
+    for g, (ref, _, row) in enumerate(main_groups):
+        level = 0 if g < 32 else (1 if g < 40 else 2)
+        add_columns(level, [(slice(row, row + 8), spread(value, g))])
+    firsts = {0: 0, 1: 12, 2: 21}
+    for dz, dy in SIDES:
+        value = both(rr[SIDE[dz, dy], 0], rr[SIDE[dz, dy], 1])
+        for level in range(3):
+            height, depth = heights[level], depths[level]
+            if dy == 0:
+                first = firsts[level] + (height // 8 if dz == 1 else 0)
+                planes = 2 if dz == 1 and level else 1
+                to = 0 if dz == 1 else (depth - 1) * height
+                for r in range(planes * height // 8):
+                    add_columns(level, [(slice(to + 8 * r, to + 8 * r + 8), spread(value, first + r))])
+                continue
+            for j in range(2 if dy == 1 and level else 1):
+                y = j if dy == 1 else height - 1
+                if level == 0:
+                    group = (10 if dy == 1 else 8) + (1 if dz else 0)
+                else:
+                    group = {1: (18, 19), 2: (24, 25)}[level][1 if dy == 1 else 0] + j
+                parts = spread(value, group)
+                if dz == 0:
+                    if level:
+                        parts = tuple(x[1:1 + depth] for x in parts)
+                    add_columns(level, [(pl.ds(y, depth, stride=height), parts)])
+                    continue
+                for p in range(2 if dz == 1 and level else 1):
+                    if level == 0:
+                        s = 1 if dz == 1 else 0
                     else:
-                        first = {"1": 256, "2": 64, "3": 16}[level]
-                        size = height
-                        to = (depth - 1) * height
-                    for r in range(0, size, 8):
-                        rows = slice(to + r, to + r + 8)
-                        ref[t, rows, :] = ref[t, rows, :] + get(level, first + r, t)
-                    continue
-                if dy == 1:
-                    blocks = {"1": ((336, 0),), "2": ((120, 0), (128, 1)), "3": ((48, 0), (56, 1))}[level]
-                else:
-                    blocks = {"1": ((320, 31),), "2": ((112, 15),), "3": ((40, 7),)}[level]
-                for first, y in blocks:
-                    if dz == 0:
-                        value = get(level, first, t)
-                        value = value if level == "1" else value[1:1 + depth]
-                        rows = pl.ds(y, depth, stride=height)
-                        ref[t, rows, :] = ref[t, rows, :] + value
-                        continue
-                    if level == "1":
-                        value = get(level, first + 8, t)
-                        pairs = ((1, 0),) if dz == 1 else ((0, depth - 1),)
-                    else:
-                        value = get(level, first, t)
-                        pairs = ((depth + 1, 0), (depth + 2, 1)) if dz == 1 else ((0, depth - 1),)
-                    for s, z in pairs:
-                        row = slice(z * height + y, z * height + y + 1)
-                        ref[t, row, :] = ref[t, row, :] + value[s:s + 1]
-
-    def arrive(d):
-        dz, dy, dx = d
-        for copy in copies(d):
-            copy.wait_recv()
-        if dx == 0:
-            def get(level, row, t):
-                if dy == 0:
-                    box = {
-                        ("1", 1): (rz1.at[0], 288), ("2", 1): (rz2u, 80), ("3", 1): (rz3u, 24),
-                        ("1", -1): (rz1.at[1], 256), ("2", -1): (rz2d, 64), ("3", -1): (rz3d, 16),
-                    }[level, dz]
-                    return box[0][t, row - box[1]:row - box[1] + 8, :]
-                first2, first3 = (120, 48) if dy == 1 else (112, 40)
-                side = SIDE[dz, dy]
-                if level == "1":
-                    return ry1[side, t, :, :]
-                if level == "2":
-                    return ry2[side, t, row - first2:row - first2 + 8, :]
-                return ry3[side, t, row - first3:row - first3 + 8, :]
-
-            add_side(dz, dy, get, lambda level: range({"1": 4, "2": 2, "3": 1}[level]))
-            return
-        keep = lane < 2 if dx == 1 else lane == 127
-        column = 0 if dx == 1 else 1
-
-        def spread(value, g):
-            moved = value if g == 0 else pltpu.roll(value, LANES - 3 * g, 1)
-            return jnp.where(keep, moved, 0.0)
-
-        if dz == 0 and dy == 0:
-            value = rxm[column]
-            for g, (ref, last, row) in enumerate(main_groups):
-                t = 0 if dx == 1 else last - 1
-                ref[t, row:row + 8, :] = ref[t, row:row + 8, :] + spread(value, g)
-            return
-        value = rxs[column, SIDE[dz, dy]]
-        add_side(
-            dz, dy,
-            lambda level, row, t: spread(value, side_index[level, row]),
-            lambda level: (0 if dx == 1 else {"1": 3, "2": 1, "3": 0}[level],),
-        )
-
-    incoming = sorted(DIRECTIONS, key=lambda d: (d[2] != 0, sum(map(abs, d)), -abs(d[1])))
-    for d in incoming:
-        @pl.when(exists(tuple(-s for s in d)))
-        def _():
-            arrive(d)
+                        s = depth + 1 + p if dz == 1 else 0
+                    z = p if dz == 1 else depth - 1
+                    row = slice(z * height + y, z * height + y + 1)
+                    add_columns(level, [(row, tuple(x[s:s + 1] for x in parts))])
 
     for z in range(8):
         for t in range(4):
@@ -451,23 +583,40 @@
     for z in range(2):
         out3[z, :, :] = l3[0, 8 * z:8 * z + 8, :]
 
-    for d in DIRECTIONS:
-        @pl.when(exists(d))
-        def _():
-            for copy in copies(d):
-                copy.wait_send()
+    for_neighbours(sent)
+
+
+def store(in1, in2, in3, out1, out2, out3, sem):
+    copies = [
+        pltpu.make_async_copy(source, target, sem.at[i])
+        for i, (source, target) in enumerate(((in1, out1), (in2, out2), (in3, out3)))
+    ]
+    for copy in copies:
+        copy.start()
+    for copy in copies:
+        copy.wait()
 
 
 def on_device(counts, volume):
+    shapes = tuple(jax.ShapeDtypeStruct(s, F32) for s in ((8, 32, 512), (4, 16, 256), (2, 8, 128)))
+    levels = levels_of(counts, shapes, volume)
+    return pl.pallas_call(
+        store,
+        out_shape=shapes,
+        in_specs=[pl.BlockSpec(memory_space=pltpu.VMEM)] * 3,
+        out_specs=[pl.BlockSpec(memory_space=pltpu.HBM)] * 3,
+        scratch_shapes=[pltpu.SemaphoreType.DMA((3,))],
+        compiler_params=pltpu.CompilerParams(vmem_limit_bytes=52 * 1024 * 1024),
+        name="store",
+    )(*levels)
+
+
+def levels_of(counts, shapes, volume):
     vmem = lambda *shape: pltpu.VMEM(shape, F32)
     return pl.pallas_call(
         functools.partial(pyramid, counts),
-        out_shape=(
-            jax.ShapeDtypeStruct((8, 32, 512), F32),
-            jax.ShapeDtypeStruct((4, 16, 256), F32),
-            jax.ShapeDtypeStruct((2, 8, 128), F32),
-        ),
-        in_specs=[pl.BlockSpec(memory_space=pl.ANY)],
+        out_shape=shapes,
+        in_specs=[pl.BlockSpec(memory_space=pltpu.HBM)],
         out_specs=[pl.BlockSpec(memory_space=pltpu.VMEM)] * 3,
         scratch_shapes=[
             vmem(16, 64, 1024),
@@ -477,16 +626,17 @@
             vmem(3, 3, 24, LANES), vmem(3, 8 * PITCH3, LANES), vmem(3, ROWS3, LANES), vmem(2, ROWS3, 256),
             vmem(2, ROWS3, LANES),
             pltpu.VMEM((256, 256), BF16), pltpu.VMEM((128, 256), BF16),
-            vmem(8, LANES), vmem(8, LANES),
+            vmem(2, 8, LANES), vmem(2, 3, 8, LANES), vmem(4, 16, LANES),
             vmem(2, 4, 32, LANES), vmem(2, 32, LANES), vmem(2, 16, LANES), vmem(1, 16, LANES), vmem(1, 8, LANES),
-            vmem(8, 4, 8, LANES), vmem(8, 2, 16, LANES), vmem(8, 1, 16, LANES),
-            vmem(2, 8, LANES), vmem(2, 8, 8, LANES),
+            vmem(2, 4, 8, LANES), vmem(2, 3, 8, LANES), vmem(4, 16, LANES),
+            vmem(2, 8, LANES), vmem(8, 2, 8, LANES),
             pltpu.SemaphoreType.DMA((4,)),
             pltpu.SemaphoreType.DMA((26, 3)),
             pltpu.SemaphoreType.DMA((26, 3)),
+            pltpu.SemaphoreType.REGULAR((2,)),
         ],
         compiler_params=pltpu.CompilerParams(
-            collective_id=0, has_side_effects=True, vmem_limit_bytes=40 * 1024 * 1024
+            collective_id=0, has_side_effects=True, vmem_limit_bytes=52 * 1024 * 1024
         ),
         name="pyramid",
     )(volume)

time: 22.5 us -> 17.3 us (0.77)
  the two profiles are of different devices: /device:TPU:75 before, /device:TPU:77 now
where the time goes in v2:
time: 17.3 us
  Pallas kernels  16.6 us (96%)
  between operations  0.64 us (4%)
    pallas_call x1, Pallas kernels, levels_of(): pl.pallas_call(functools.partial(pyramid, counts), out_shape=shapes, in_s...  15.8 us
    pallas_call x1, Pallas kernels, on_device(): pl.pallas_call(store, out_shape=shapes, in_specs=[pl.BlockSpec(memory_spa...  0.83 us

profile of v2, /device:TPU:77, one launch (start us, length us, event | category | flops | bytes accessed | tf_op | source)
XLA Modules:
  0.0 17.3 jit_solution(8022589831803053821)
XLA Ops:
  0.6 15.8 %pyramid.1 = (f32[8,32,512]{2,1,0:T(8,128)S(1)}, f32[4,16,256]{2,1,0:T(8,128)S(1)}, f32[2,8,128]{2,1,0:T(8,128)S(1)}) custom-call(f32[16,64,1024]{2,1,0:T(8,128)} %vol.1), custom_call_target="tpu_custom_call" | custom-call | tf_op jit(solution)/shard_map/pyramid/pallas_call | solution.py:616
  16.4 0.8 %store.1 = (f32[8,32,512]{2,1,0:T(8,128)}, f32[4,16,256]{2,1,0:T(8,128)}, f32[2,8,128]{2,1,0:T(8,128)}) custom-call(f32[8,32,512]{2,1,0:T(8,128)S(1)} %get-tuple-element.6.in1, f32[4,16,256]{2,1,0:T(8,128)S(1)} %get-tuple-element.7.in2, f32[2,8,128]{2,1,0:T(8,128)S(1)} %get-tuple-element.8.in3), custom_call_target="tpu_custom_call" | custom-call | tf_op jit(solution)/shard_map/store/pallas_call | solution.py:603

commit v3 on v2

--- a/solution.py
+++ b/solution.py
@@ -28,6 +28,7 @@
 UPPER = [d for d in DIRECTIONS if (d[2], d[1], d[0]) > (0, 0, 0)]
 LOWER = [d for d in DIRECTIONS if (d[2], d[1], d[0]) < (0, 0, 0)]
 FACES = [(1, 0, 0), (-1, 0, 0), (0, 1, 0), (0, -1, 0)]
+GROUP = {0: (0, 0), 3: (0, 1), 1: (1, 0), 2: (1, 1)}
 CORNER = {(1, 1): 0, (1, -1): 1, (-1, 1): 2, (-1, -1): 3}
 
 
@@ -85,8 +86,38 @@
     edge[...] = jnp.where(legal, value * (1.0 / 4096.0), 0.0).astype(BF16)
 
 
-def pyramid(counts, vol, out1, out2, out3, v, zs1, as1, p1, l1, ye1, zs2, as2, p2, l2, ye2, zs3, as3, p3, l3,
-            band, edge, xp, yf, q, rz1, rz2u, rz2d, rz3u, rz3d, ry1, ryf, rq, rx, rr,
+def build_end_weights(ends1, ends2, ends3):
+    tap1 = [6, 4, 1]
+    tap2 = [44, 40, 31, 20, 10, 4, 1]
+    tap3 = [344, 336, 315, 284, 246, 204, 161, 120, 84, 56, 35, 20, 10, 4, 1]
+    k = lax.broadcasted_iota(jnp.int32, (32, LANES), 0) - 16
+    lane = lax.broadcasted_iota(jnp.int32, (32, LANES), 1)
+    zero = jnp.zeros((112, LANES), BF16)
+
+    def fill(ref, value):
+        ref[0:112, :] = zero
+        ref[112:144, :] = value.astype(BF16)
+        ref[144:256, :] = zero
+
+    for level, taps_of in enumerate((tap1, tap2, tap3)):
+        step = 2 << level
+        high = jnp.where((k < 0) & (lane < 2), step * lane - k, 99)
+        distance = jnp.where((k >= 0) & (lane == 127), k + step, high)
+        scale = 1.0 / 4096.0 ** (level + 1)
+        value = jnp.zeros((32, LANES), F32)
+        for offset, tap in enumerate(taps_of):
+            value = jnp.where(distance == offset, (316 if tap == 315 else tap) * scale, value)
+        if level == 0:
+            fill(ends1, value)
+        elif level == 1:
+            fill(ends2, value)
+        else:
+            fill(ends3.at[0], value)
+            fill(ends3.at[1], jnp.where(distance == 2, -scale, 0.0))
+
+
+def pyramid(counts, vol, out1, out2, out3, v, zs1, as1, cut1, p1, l1, ye1, zs2, as2, p2, l2, ye2, zs3, as3, p3, l3,
+            band, edge, ends1, ends2, ends3, x1, x2, x3, xp, yf, q, rz1, rz2u, rz2d, rz3u, rz3d, ry1, ryf, rq, rx, rr,
             load_sem, send_sem, recv_sem, ready):
     me = {axis: lax.axis_index(axis) for axis in ("gz", "gy", "gx")}
     has = {(axis, 1): me[axis] < counts[axis] - 1 for axis in me}
@@ -123,15 +154,15 @@
             for r in range(0, target.shape[0], 8):
                 target[r:r + 8, :] = zeros
 
-    order = (0, 3, 1, 2)
+    pieces = ((0, 1), (7, 1), (1, 1), (6, 1), (2, 2), (4, 2))
     loads = [
         pltpu.make_async_copy(
-            vol.at[:, :, pl.ds(256 * b, 256)], v.at[:, :, pl.ds(256 * b, 256)], load_sem.at[b]
+            vol.at[:, :, pl.ds(LANES * c, LANES * n)], v.at[:, :, pl.ds(LANES * c, LANES * n)], load_sem.at[i]
         )
-        for b in range(4)
+        for i, (c, n) in enumerate(pieces)
     ]
-    for b in order:
-        loads[b].start()
+    for load in loads:
+        load.start()
 
     barrier = pltpu.get_barrier_semaphore()
     interior = functools.reduce(lambda x, y: x & y, has.values())
@@ -157,6 +188,7 @@
                 blank(d)
 
     build_weights(band, edge)
+    build_end_weights(ends1, ends2, ends3)
     zero8 = jnp.zeros((8, LANES), F32)
     for c in range(8):
         for p in range(11):
@@ -169,7 +201,7 @@
     for side in range(2):
         for t in range(3):
             yf[side, t] = zero8
-    for t in range(5):
+    for t in range(7):
         for e in range(2):
             for r in range(0, 24, 8):
                 ye1[t, e, r:r + 8, :] = zero8
@@ -179,7 +211,7 @@
         for r in range(8, 40, 8):
             zs2[t, 7 * PITCH2 + r:7 * PITCH2 + r + 8, :] = zero8
         as2[t, 136:144, :] = zero8
-    for t in range(3):
+    for t in range(5):
         for e in range(3):
             for r in range(0, 24, 8):
                 ye2[t, e, r:r + 8, :] = zero8
@@ -258,24 +290,38 @@
 
     start, received, sent = (lambda c: c.start()), (lambda c: c.wait_recv()), (lambda c: c.wait_send())
 
-    def level_one_tiles(b):
+    zflag2 = jnp.where(sub == 0, zlo, jnp.where(sub < 5, 1.0, zhi))
+    plane_row1 = lambda s: 256 if s == -1 else (288 if s == 8 else 32 * s)
+    plane_row2 = lambda s: 64 if s == -1 else (80 + 16 * (s - 4) if s >= 4 else 16 * s)
+    plane_row3 = lambda s: 16 if s == -1 else (24 + 8 * (s - 2) if s >= 2 else 8 * s)
+    zscale2 = lambda i: zlo if i == -1 else (zhi if i >= 4 else None)
+
+    def cut(c, row, block):
+        group, place = GROUP[c // 2]
+        at = place * ROWS1 + row
+        for piece, value in enumerate(split(block)):
+            cut1[group, piece, at:at + block.shape[0], LANES * (c % 2):LANES * (c % 2) + LANES] = value
+
+    def level_one_tiles(c, n):
         for r in range(0, 64, 8):
-            planes = [v[s, r:r + 8, 256 * b:256 * b + 256] for s in range(16)]
+            planes = [v[s, r:r + 8, LANES * c:LANES * (c + n)] for s in range(16)]
             for i in range(-1, 9):
                 plane = reduce_planes(lambda s: planes[s], 0, 15, i)
                 row = (i + 1) * PITCH1 + 8 + r
-                for h in range(2):
-                    zs1[2 * b + h, row:row + 8, :] = plane[:, 128 * h:128 * h + 128]
-        for c in (2 * b, 2 * b + 1):
+                for h in range(n):
+                    zs1[c + h, row:row + 8, :] = plane[:, LANES * h:LANES * h + LANES]
+        for c in range(c, c + n):
             for i in range(-1, 9):
                 base = (i + 1) * PITCH1 + 8
                 plane = weighted({k: zs1[c, pl.ds(base + k - 2, 32, stride=2), :] for k in range(5)})
                 if i == -1:
-                    as1[c, 256:288, :] = plane * zlo
+                    plane = plane * zlo
                 elif i == 8:
-                    as1[c, 288:320, :] = plane * zhi
-                else:
-                    as1[c, 32 * i:32 * i + 32, :] = plane
+                    plane = plane * zhi
+                row = plane_row1(i)
+                if c in (0, 7):
+                    as1[c, row:row + 32, :] = plane
+                cut(c, row, plane)
 
             def column(y, p, size):
                 return zs1[c, pl.ds(p * PITCH1 + 8 + y, size, stride=PITCH1), :]
@@ -288,10 +334,70 @@
                 as1[c, 344 + s:345 + s, :] = weighted(
                     {0: zs1[c, first + 62:first + 63, :], 1: zs1[c, first + 63:first + 64, :]}
                 ) * (yhi * zflag)
-        for r in range(0, ROWS1, 176):
-            rows = slice(r, r + 176)
-            block = jnp.concatenate([as1[2 * b, rows, :], as1[2 * b + 1, rows, :]], axis=1)
-            p1[b, rows, :] = product(block, band[...])
+            cut(c, 320, as1[c, 320:352, :])
+
+    def level_one_product(blocks):
+        group = GROUP[blocks[0]][0]
+        total = None
+        for piece in range(3):
+            part = jnp.dot(cut1[group, piece], band[...], preferred_element_type=F32)
+            total = part if total is None else total + part
+        for b in blocks:
+            at = GROUP[b][1] * ROWS1
+            p1[b] = total[at:at + ROWS1]
+
+    def level_two_tile(source, t):
+        for e, first in ((0, 320), (1, 336)):
+            ye1[t, e, 8:16, :] = source[first:first + 8, :]
+            ye1[t, e, 7:8, :] = source[first + 8:first + 9, :]
+            ye1[t, e, 16:17, :] = source[first + 9:first + 10, :]
+        for i in range(-1, 6):
+            plane = reduce_planes(lambda s: source[plane_row1(s):plane_row1(s) + 32, :], -1, 8, i)
+            if zscale2(i) is not None:
+                plane = plane * zscale2(i)
+            row = (i + 1) * PITCH2 + 8
+            zs2[t, row:row + 32, :] = plane
+        for e, y in ((0, -1), (1, 32)):
+            block = weighted({k: ye1[t, e, pl.ds(4 + k, 8, stride=2), :] for k in range(5)})
+            zs2[t, pl.ds(8 + y, 8, stride=PITCH2), :] = block * zflag2
+        for i in range(-1, 6):
+            base = (i + 1) * PITCH2 + 8
+            row = plane_row2(i)
+            as2[t, row:row + 16, :] = weighted(
+                {k: zs2[t, pl.ds(base + k - 2, 16, stride=2), :] for k in range(5)}
+            )
+
+        def column2(y):
+            return zs2[t, pl.ds(8 + y, 8, stride=PITCH2), :]
+
+        as2[t, 112:120, :] = weighted({3: column2(-1), 4: column2(0)}) * ylo
+        as2[t, 120:128, :] = weighted({0: column2(30), 1: column2(31), 2: column2(32)}) * yhi
+        as2[t, 128:136, :] = column2(32) * yhi
+
+    def level_three_tile(source, t):
+        for e, first in ((0, 112), (1, 120), (2, 128)):
+            ye2[t, e, 7:15, :] = source[first:first + 8, :]
+        for i in range(-1, 4):
+            row = (i + 1) * PITCH3 + 8
+            zs3[t, row:row + 16, :] = reduce_planes(
+                lambda s: source[plane_row2(s):plane_row2(s) + 16, :], -1, 5, i
+            )
+        for e, y in ((0, -1), (1, 16), (2, 17)):
+            block = weighted({k: ye2[t, e, pl.ds(4 + k, 8, stride=2), :] for k in range(5)})
+            zs3[t, pl.ds(8 + y, 8, stride=PITCH3), :] = block
+        for i in range(-1, 4):
+            base = (i + 1) * PITCH3 + 8
+            row = plane_row3(i)
+            as3[t, row:row + 8, :] = weighted(
+                {k: zs3[t, pl.ds(base + k - 2, 8, stride=2), :] for k in range(5)}
+            )
+
+        def column3(y):
+            return zs3[t, pl.ds(8 + y, 8, stride=PITCH3), :]
+
+        as3[t, 40:48, :] = weighted({3: column3(-1), 4: column3(0)})
+        as3[t, 48:56, :] = weighted({k: column3(14 + k) for k in range(4)})
+        as3[t, 56:64, :] = weighted({0: column3(16), 1: column3(17)})
 
     def combine(parts, result, tiles, rows, mask):
         size = 16
@@ -314,14 +420,41 @@
                     value = value * wide
                 result[t, r:r + size, :] = value
 
-    for b in order:
-        loads[b].wait()
-        level_one_tiles(b)
-
-    def parts1(t, r, size, half):
-        return None if t == 4 else p1[t, r:r + size, 128 * half:128 * half + 128]
-
-    combine(parts1, l1, 4, ROWS1, xflag)
+    main_groups = [(l1, 4, 8 * g) for g in range(32)] + [(l2, 2, 8 * g) for g in range(8)] + [(l3, 1, 8 * g) for g in range(2)]
+    main_rows = [(x1, 8 * g) for g in range(32)] + [(x2, 8 * g) for g in range(8)] + [(x3, 8 * g) for g in range(2)]
+    side_rows = (
+        [(x1, 256 + 8 * g) for g in range(12)] + [(x2, 64 + 8 * g) for g in range(9)] + [(x3, 16 + 8 * g) for g in range(6)]
+    )
+
+    def pack(groups):
+        total = None
+        for g, (ref, row) in enumerate(groups):
+            piece = ref[row:row + 8, :]
+            piece = piece if g == 0 else pltpu.roll(piece, 3 * g, 1)
+            total = piece if total is None else total + piece
+        return total
+
+    def ends(source, high, low):
+        return jnp.concatenate([source[high], source[low]], axis=1)
+
+    for i in range(2):
+        loads[i].wait()
+        level_one_tiles(*pieces[i])
+    for i in range(2, 4):
+        loads[i].wait()
+    level_one_tiles(*pieces[2])
+    level_one_tiles(*pieces[3])
+    level_one_product((0, 3))
+    level_two_tile(as1.at[0], 5)
+    level_two_tile(as1.at[7], 6)
+    level_three_tile(as2.at[5], 3)
+    level_three_tile(as2.at[6], 4)
+    x1[...] = product(ends(as1, 7, 0), ends1[...])
+    x2[...] = product(ends(as2, 6, 5), ends2[...])
+    block = ends(as3, 4, 3)
+    x3[...] = product(block, ends3[0]) + product(block, ends3[1])
+    xp[0] = pack(main_rows)
+    xp[1] = pack(side_rows)
     one = {key: value.astype(jnp.int32) for key, value in has.items()}
     across_z = 1 + one["gz", 1] + one["gz", -1]
     across = across_z * (1 + one["gy", 1] + one["gy", -1])
@@ -333,56 +466,50 @@
         def _():
             pl.semaphore_wait(semaphore, number)
 
-    wait_for(barrier, near_lower + far_lower)
-
     def answer(d):
         signal(ready.at[1 if d[2] else 0], d)
 
-    @pl.when(interior)
+
+    def enter():
+        wait_for(barrier, near_lower + far_lower)
+
+        @pl.when(interior)
+        def _():
+            for d in LOWER:
+                answer(d)
+
+        @pl.when(jnp.logical_not(interior))
+        def _():
+            for d in LOWER:
+                @pl.when(exists(d))
+                def _():
+                    answer(d)
+
+    last_column = jnp.logical_not(has["gx", 1])
+
+    @pl.when(jnp.logical_not(last_column))
     def _():
-        for d in LOWER:
-            answer(d)
-
-    @pl.when(jnp.logical_not(interior))
+        enter()
+        for_neighbours(start, (2,), only=[d for d in LOWER if d[2]])
+
+    for i in range(4, 6):
+        loads[i].wait()
+    level_one_tiles(*pieces[4])
+    @pl.when(last_column)
     def _():
-        for d in LOWER:
-            @pl.when(exists(d))
-            def _():
-                answer(d)
-
+        enter()
+        for_neighbours(start, (2,), only=[d for d in LOWER if d[2]])
+
+    level_one_tiles(*pieces[5])
+    level_one_product((1, 2))
+
+    def parts1(t, r, size, half):
+        return None if t == 4 else p1[t, r:r + size, 128 * half:128 * half + 128]
+
+    combine(parts1, l1, 4, ROWS1, xflag)
     for_neighbours(start, (0,), only=LOWER)
-    zflag2 = jnp.where(sub == 0, zlo, jnp.where(sub < 5, 1.0, zhi))
-    plane_row1 = lambda s: 256 if s == -1 else (288 if s == 8 else 32 * s)
-    plane_row2 = lambda s: 64 if s == -1 else (80 + 16 * (s - 4) if s >= 4 else 16 * s)
-    plane_row3 = lambda s: 16 if s == -1 else (24 + 8 * (s - 2) if s >= 2 else 8 * s)
-    zscale2 = lambda i: zlo if i == -1 else (zhi if i >= 4 else None)
     for t in range(5):
-        for e, first in ((0, 320), (1, 336)):
-            ye1[t, e, 8:16, :] = l1[t, first:first + 8, :]
-            ye1[t, e, 7:8, :] = l1[t, first + 8:first + 9, :]
-            ye1[t, e, 16:17, :] = l1[t, first + 9:first + 10, :]
-        for i in range(-1, 6):
-            plane = reduce_planes(lambda s: l1[t, plane_row1(s):plane_row1(s) + 32, :], -1, 8, i)
-            if zscale2(i) is not None:
-                plane = plane * zscale2(i)
-            row = (i + 1) * PITCH2 + 8
-            zs2[t, row:row + 32, :] = plane
-        for e, y in ((0, -1), (1, 32)):
-            block = weighted({k: ye1[t, e, pl.ds(4 + k, 8, stride=2), :] for k in range(5)})
-            zs2[t, pl.ds(8 + y, 8, stride=PITCH2), :] = block * zflag2
-        for i in range(-1, 6):
-            base = (i + 1) * PITCH2 + 8
-            row = plane_row2(i)
-            as2[t, row:row + 16, :] = weighted(
-                {k: zs2[t, pl.ds(base + k - 2, 16, stride=2), :] for k in range(5)}
-            )
-
-        def column2(y):
-            return zs2[t, pl.ds(8 + y, 8, stride=PITCH2), :]
-
-        as2[t, 112:120, :] = weighted({3: column2(-1), 4: column2(0)}) * ylo
-        as2[t, 120:128, :] = weighted({0: column2(30), 1: column2(31), 2: column2(32)}) * yhi
-        as2[t, 128:136, :] = column2(32) * yhi
+        level_two_tile(l1.at[t], t)
     for b in range(2):
         block = jnp.concatenate([as2[2 * b], as2[2 * b + 1]], axis=1)
         p2[b] = product(block, band[...])
@@ -395,29 +522,7 @@
     for_neighbours(start, (1,), only=LOWER)
 
     for t in range(3):
-        for e, first in ((0, 112), (1, 120), (2, 128)):
-            ye2[t, e, 7:15, :] = l2[t, first:first + 8, :]
-        for i in range(-1, 4):
-            row = (i + 1) * PITCH3 + 8
-            zs3[t, row:row + 16, :] = reduce_planes(
-                lambda s: l2[t, plane_row2(s):plane_row2(s) + 16, :], -1, 5, i
-            )
-        for e, y in ((0, -1), (1, 16), (2, 17)):
-            block = weighted({k: ye2[t, e, pl.ds(4 + k, 8, stride=2), :] for k in range(5)})
-            zs3[t, pl.ds(8 + y, 8, stride=PITCH3), :] = block
-        for i in range(-1, 4):
-            base = (i + 1) * PITCH3 + 8
-            row = plane_row3(i)
-            as3[t, row:row + 8, :] = weighted(
-                {k: zs3[t, pl.ds(base + k - 2, 8, stride=2), :] for k in range(5)}
-            )
-
-        def column3(y):
-            return zs3[t, pl.ds(8 + y, 8, stride=PITCH3), :]
-
-        as3[t, 40:48, :] = weighted({3: column3(-1), 4: column3(0)})
-        as3[t, 48:56, :] = weighted({k: column3(14 + k) for k in range(4)})
-        as3[t, 56:64, :] = weighted({0: column3(16), 1: column3(17)})
+        level_three_tile(l2.at[t], t)
     p3[0] = product(jnp.concatenate([as3[0], as3[1]], axis=1), band[...])
     p3[1] = product(as3[2], edge[...])
 
@@ -425,17 +530,6 @@
         return p3[t, r:r + size, 128 * half:128 * half + 128]
 
     combine(parts3, l3, 1, ROWS3, None)
-
-    main_groups = [(l1, 4, 8 * g) for g in range(32)] + [(l2, 2, 8 * g) for g in range(8)] + [(l3, 1, 8 * g) for g in range(2)]
-    side_groups = [(l1, 4, 256 + 8 * g) for g in range(12)] + [(l2, 2, 64 + 8 * g) for g in range(9)] + [(l3, 1, 16 + 8 * g) for g in range(6)]
-
-    def pack(groups):
-        total = None
-        for g, (ref, t, row) in enumerate(groups):
-            piece = ref[t, row:row + 8, :]
-            piece = piece if g == 0 else pltpu.roll(piece, 3 * g, 1)
-            total = piece if total is None else total + piece
-        return total
 
     for side, blocks2, blocks3 in ((0, (120, 128), (48, 56)), (1, (112,), (40,))):
         for t in range(2):
@@ -456,10 +550,8 @@
             for j, row in enumerate(blocks3):
                 q[corner, 4 + 2 * j:4 + 2 * j + size, :] = l3[0, row + first3:row + first3 + size, :]
 
-    xp[0] = pack(main_groups)
-    xp[1] = pack(side_groups)
-
-    for_neighbours(start, (2,), only=LOWER)
+
+    for_neighbours(start, (2,), only=[d for d in LOWER if not d[2]])
     wait_for(ready.at[0], near_upper)
     for_neighbours(start, only=[d for d in UPPER if d[2] == 0])
     wait_for(ready.at[1], far_upper)
@@ -517,6 +609,7 @@
         add_z(-1, 1, t, lambda r: rz2d[t, r:r + 8, :])
     add_z(1, 2, 0, lambda r: rz3u[0, r:r + 8, :])
     add_z(-1, 2, 0, lambda r: rz3d[0, r:r + 8, :])
+    for_neighbours(sent)
     for_neighbours(received, back=True, only=[d for d in DIRECTIONS if d[2]])
     third = lax.rem(lane, 3)
     low_lanes, high_lane = lane < 2, lane == 127
@@ -583,8 +676,6 @@
     for z in range(2):
         out3[z, :, :] = l3[0, 8 * z:8 * z + 8, :]
 
-    for_neighbours(sent)
-
 
 def store(in1, in2, in3, out1, out2, out3, sem):
     copies = [
@@ -620,17 +711,20 @@
         out_specs=[pl.BlockSpec(memory_space=pltpu.VMEM)] * 3,
         scratch_shapes=[
             vmem(16, 64, 1024),
-            vmem(8, 10 * PITCH1 + 8, LANES), vmem(8, ROWS1, LANES), vmem(4, ROWS1, 256), vmem(5, ROWS1, LANES),
-            vmem(5, 2, 24, LANES), vmem(5, 8 * PITCH2, LANES), vmem(5, ROWS2, LANES), vmem(3, ROWS2, 256),
+            vmem(8, 10 * PITCH1 + 8, LANES), vmem(8, ROWS1, LANES),
+            pltpu.VMEM((2, 3, 2 * ROWS1, 256), BF16), vmem(4, ROWS1, 256), vmem(5, ROWS1, LANES),
+            vmem(7, 2, 24, LANES), vmem(7, 8 * PITCH2, LANES), vmem(7, ROWS2, LANES), vmem(3, ROWS2, 256),
             vmem(3, ROWS2, LANES),
-            vmem(3, 3, 24, LANES), vmem(3, 8 * PITCH3, LANES), vmem(3, ROWS3, LANES), vmem(2, ROWS3, 256),
+            vmem(5, 3, 24, LANES), vmem(5, 8 * PITCH3, LANES), vmem(5, ROWS3, LANES), vmem(2, ROWS3, 256),
             vmem(2, ROWS3, LANES),
             pltpu.VMEM((256, 256), BF16), pltpu.VMEM((128, 256), BF16),
+            pltpu.VMEM((256, LANES), BF16), pltpu.VMEM((256, LANES), BF16), pltpu.VMEM((2, 256, LANES), BF16),
+            vmem(ROWS1, LANES), vmem(ROWS2, LANES), vmem(ROWS3, LANES),
             vmem(2, 8, LANES), vmem(2, 3, 8, LANES), vmem(4, 16, LANES),
             vmem(2, 4, 32, LANES), vmem(2, 32, LANES), vmem(2, 16, LANES), vmem(1, 16, LANES), vmem(1, 8, LANES),
             vmem(2, 4, 8, LANES), vmem(2, 3, 8, LANES), vmem(4, 16, LANES),
             vmem(2, 8, LANES), vmem(8, 2, 8, LANES),
-            pltpu.SemaphoreType.DMA((4,)),
+            pltpu.SemaphoreType.DMA((6,)),
             pltpu.SemaphoreType.DMA((26, 3)),
             pltpu.SemaphoreType.DMA((26, 3)),
             pltpu.SemaphoreType.REGULAR((2,)),

time: 17.3 us -> 15.6 us (0.902)
  the two profiles are of different devices: /device:TPU:77 before, /device:TPU:235 now
where the time goes in v3:
time: 15.6 us; the launch traced here: 15.5 us
  Pallas kernels  14.8 us (95%)
  between operations  0.64 us (4%)
    pallas_call x1, Pallas kernels, levels_of(): pl.pallas_call(functools.partial(pyramid, counts), out_shape=shapes, in_s...  14 us
    pallas_call x1, Pallas kernels, on_device(): pl.pallas_call(store, out_shape=shapes, in_specs=[pl.BlockSpec(memory_spa...  0.83 us

profile of v3, /device:TPU:235, one launch (start us, length us, event | category | flops | bytes accessed | tf_op | source)
XLA Modules:
  0.0 15.5 jit_solution(17742957503714127321)
XLA Ops:
  0.6 14.0 %pyramid.1 = (f32[8,32,512]{2,1,0:T(8,128)S(1)}, f32[4,16,256]{2,1,0:T(8,128)S(1)}, f32[2,8,128]{2,1,0:T(8,128)S(1)}) custom-call(f32[16,64,1024]{2,1,0:T(8,128)} %vol.1), custom_call_target="tpu_custom_call" | custom-call | tf_op jit(solution)/shard_map/pyramid/pallas_call | solution.py:707
  14.6 0.8 %store.1 = (f32[8,32,512]{2,1,0:T(8,128)}, f32[4,16,256]{2,1,0:T(8,128)}, f32[2,8,128]{2,1,0:T(8,128)}) custom-call(f32[8,32,512]{2,1,0:T(8,128)S(1)} %get-tuple-element.6.in1, f32[4,16,256]{2,1,0:T(8,128)S(1)} %get-tuple-element.7.in2, f32[2,8,128]{2,1,0:T(8,128)S(1)} %get-tuple-element.8.in3), custom_call_target="tpu_custom_call" | custom-call | tf_op jit(solution)/shard_map/store/pallas_call | solution.py:694

commit v4 on v3

--- a/solution.py
+++ b/solution.py
@@ -1,4 +1,5 @@
 import functools
+import math
 
 import jax
 import jax.numpy as jnp
@@ -11,6 +12,7 @@
 F32 = jnp.float32
 BF16 = jnp.bfloat16
 LANES = 128
+AXES = ("gz", "gy", "gx")
 taps = (1.0, 4.0, 6.0, 4.0, 1.0)
 
 ROWS1, ROWS2, ROWS3 = 352, 144, 64
@@ -22,11 +24,13 @@
     for dy in (-1, 1, 0)
     if (dz, dy, dx) != (0, 0, 0)
 ]
-SLOT = {d: i for i, d in enumerate(DIRECTIONS)}
-SIDES = [(dz, dy) for dz in (1, -1, 0) for dy in (1, -1, 0) if (dz, dy) != (0, 0)]
+SIDES = [(1, -1), (-1, -1), (0, -1), (-1, 0), (1, 1), (-1, 1), (0, 1), (1, 0)]
 SIDE = {d: i for i, d in enumerate(SIDES)}
 UPPER = [d for d in DIRECTIONS if (d[2], d[1], d[0]) > (0, 0, 0)]
 LOWER = [d for d in DIRECTIONS if (d[2], d[1], d[0]) < (0, 0, 0)]
+TARGETS = [d for d in DIRECTIONS if d[2] < 1 or d == (0, 0, 1)]
+NEAR_LOWER, NEAR_UPPER = ([d for d in half if not d[2]] for half in (LOWER, UPPER))
+FAR_LOWER, NEXT, BEFORE = [d for d in LOWER if d[2]], (0, 0, 1), (0, 0, -1)
 FACES = [(1, 0, 0), (-1, 0, 0), (0, 1, 0), (0, -1, 0)]
 GROUP = {0: (0, 0), 3: (0, 1), 1: (1, 0), 2: (1, 1)}
 CORNER = {(1, 1): 0, (1, -1): 1, (-1, 1): 2, (-1, -1): 3}
@@ -117,7 +121,7 @@
 
 
 def pyramid(counts, vol, out1, out2, out3, v, zs1, as1, cut1, p1, l1, ye1, zs2, as2, p2, l2, ye2, zs3, as3, p3, l3,
-            band, edge, ends1, ends2, ends3, x1, x2, x3, xp, yf, q, rz1, rz2u, rz2d, rz3u, rz3d, ry1, ryf, rq, rx, rr,
+            band, edge, ends1, ends2, ends3, x1, x2, x3, xp, yf, q, rz1, rz2u, rz2d, rz3u, rz3d, ry1, ryf, rq, rx, ru, rru, rrd,
             load_sem, send_sem, recv_sem, ready):
     me = {axis: lax.axis_index(axis) for axis in ("gz", "gy", "gx")}
     has = {(axis, 1): me[axis] < counts[axis] - 1 for axis in me}
@@ -136,11 +140,16 @@
     def blank(d):
         dz, dy, dx = d
         zeros = jnp.zeros((8, LANES), F32)
+        if d == NEXT:
+            rx[0] = zeros
+            for i in range(8):
+                rru[i] = zeros
+            return
         if dx:
-            column = 0 if dx == 1 else 1
-            target = rr.at[SIDE[dz, dy], column] if dz or dy else rx.at[column]
+            target = rrd.at[SIDE[dz, dy]] if dz or dy else rx.at[1]
             target[...] = zeros
             return
+        ru[SIDE[dz, dy]] = zeros
         side = 0 if dy == 1 else 1
         if dz and dy:
             targets = [rq.at[CORNER[dz, dy]]]
@@ -182,7 +191,7 @@
             def _():
                 signal(barrier, d)
 
-        for d in DIRECTIONS:
+        for d in TARGETS:
             @pl.when(jnp.logical_not(exists(tuple(-k for k in d))))
             def _():
                 blank(d)
@@ -231,39 +240,53 @@
 
     def transfers(d):
         dz, dy, dx = d
-        if dx:
-            column = 0 if dx == 1 else 1
-            if dz == 0 and dy == 0:
-                return {2: (xp.at[0], rx.at[column])}
-            return {2: (xp.at[1], rr.at[SIDE[dz, dy], column])}
+        if dx == 1:
+            return {
+                2: (xp.at[0], rx.at[0]),
+                4: (ru.at[pl.ds(0, 4)], rru.at[pl.ds(0, 4)]),
+                5: (ru.at[pl.ds(4, 4)], rru.at[pl.ds(4, 4)]),
+            }
+        if dx == -1:
+            return {2: (xp.at[1], rrd.at[SIDE[dz, dy]]) if dz or dy else (xp.at[0], rx.at[1])}
+        along = (xp.at[1], ru.at[SIDE[dz, dy]])
         if dy == 0:
             if dz == 1:
                 return {
                     0: (l1.at[pl.ds(0, 4), pl.ds(288, 32), :], rz1.at[0]),
                     1: (l2.at[pl.ds(0, 2), pl.ds(80, 32), :], rz2u),
                     2: (l3.at[pl.ds(0, 1), pl.ds(24, 16), :], rz3u),
+                    3: along,
                 }
             return {
                 0: (l1.at[pl.ds(0, 4), pl.ds(256, 32), :], rz1.at[1]),
                 1: (l2.at[pl.ds(0, 2), pl.ds(64, 16), :], rz2d),
                 2: (l3.at[pl.ds(0, 1), pl.ds(16, 8), :], rz3d),
+                3: along,
             }
         if dz == 0:
             side = 0 if dy == 1 else 1
             return {
                 0: (l1.at[pl.ds(0, 4), pl.ds(336 if dy == 1 else 320, 8), :], ry1.at[side]),
                 2: (yf.at[side], ryf.at[side]),
+                3: along,
             }
         corner = CORNER[dz, dy]
-        return {2: (q.at[corner], rq.at[corner])}
-
-    def copies(d, stages=(0, 1, 2)):
+        return {2: (q.at[corner], rq.at[corner]), 3: along}
+
+    def awaited_with(d, stage):
+        if d[2]:
+            return 0
+        if stage == 3:
+            return 1 if d in NEAR_LOWER else 2
+        return 3 if d[1] else 4
+
+    def copies(d, stages=(0, 1, 2, 3, 4, 5)):
         return [
             pltpu.make_async_remote_copy(
                 src_ref=pair[0],
                 dst_ref=pair[1],
-                send_sem=send_sem.at[SLOT[d], i],
-                recv_sem=recv_sem.at[SLOT[d], i],
+                send_sem=send_sem.at[0 if d[2] or i == 3 else 1],
+                recv_sem=recv_sem.at[awaited_with(d, i)],
                 device_id=device(d),
                 device_id_type=MESH,
             )
@@ -271,8 +294,8 @@
             if i in stages
         ]
 
-    def for_neighbours(act, stages=(0, 1, 2), back=False, only=None):
-        chosen = [d for d in (only or DIRECTIONS) if any(i in stages for i in transfers(d))]
+    def for_neighbours(act, stages=(0, 1, 2, 3, 4, 5), back=False, only=None):
+        chosen = [d for d in (only or TARGETS) if any(i in stages for i in transfers(d))]
 
         @pl.when(interior)
         def _():
@@ -288,7 +311,45 @@
                     for copy in copies(d, stages):
                         act(copy)
 
-    start, received, sent = (lambda c: c.start()), (lambda c: c.wait_recv()), (lambda c: c.wait_send())
+    start = lambda c: c.start()
+
+    def settle(semaphore, only, stages, back):
+        parts = []
+        for d in only:
+            units = sum(
+                math.prod(pair[0].shape) // 1024
+                for i, pair in transfers(d).items()
+                if (i in stages if stages else d[2] or i == 3)
+            )
+            parts.append((tuple(-k for k in d) if back else d, units))
+        axes = [a for j, a in enumerate(AXES) if any(d[j] for d, _ in parts)]
+
+        def wait(state):
+            units = sum(u for d, u in parts if all(state[a, k] for a, k in zip(AXES, d) if k))
+            if units:
+                rows = pl.ds(0, 8 * units)
+                pltpu.make_async_copy(zs1.at[0, rows, :], zs1.at[1, rows, :], semaphore).wait()
+
+        def choose(left, state):
+            if not left:
+                wait(state)
+                return
+            axis = left[0]
+            for low, high in ((True, True), (True, False), (False, True)):
+                fits = has[axis, -1] if low else jnp.logical_not(has[axis, -1])
+                fits &= has[axis, 1] if high else jnp.logical_not(has[axis, 1])
+
+                @pl.when(fits)
+                def _():
+                    choose(left[1:], {**state, (axis, -1): low, (axis, 1): high})
+
+        @pl.when(interior)
+        def _():
+            wait({(a, k): True for a in AXES for k in (-1, 1)})
+
+        @pl.when(jnp.logical_not(interior))
+        def _():
+            choose(axes, {})
 
     zflag2 = jnp.where(sub == 0, zlo, jnp.where(sub < 5, 1.0, zhi))
     plane_row1 = lambda s: 256 if s == -1 else (288 if s == 8 else 32 * s)
@@ -459,7 +520,7 @@
     across_z = 1 + one["gz", 1] + one["gz", -1]
     across = across_z * (1 + one["gy", 1] + one["gy", -1])
     near_lower, near_upper = (one["gy", k] * across_z + one["gz", k] for k in (-1, 1))
-    far_lower, far_upper = (one["gx", k] * across for k in (-1, 1))
+    far_lower, far_upper = one["gx", -1] * across, one["gx", 1]
 
     def wait_for(semaphore, number):
         @pl.when(number > 0)
@@ -475,22 +536,24 @@
 
         @pl.when(interior)
         def _():
-            for d in LOWER:
+            for d in [BEFORE] + NEAR_LOWER:
                 answer(d)
 
         @pl.when(jnp.logical_not(interior))
         def _():
-            for d in LOWER:
+            for d in [BEFORE] + NEAR_LOWER:
                 @pl.when(exists(d))
                 def _():
                     answer(d)
 
+        for_neighbours(start, (2,), only=FAR_LOWER)
+        for_neighbours(start, (3,), only=NEAR_LOWER)
+
     last_column = jnp.logical_not(has["gx", 1])
 
     @pl.when(jnp.logical_not(last_column))
     def _():
         enter()
-        for_neighbours(start, (2,), only=[d for d in LOWER if d[2]])
 
     for i in range(4, 6):
         loads[i].wait()
@@ -498,7 +561,6 @@
     @pl.when(last_column)
     def _():
         enter()
-        for_neighbours(start, (2,), only=[d for d in LOWER if d[2]])
 
     level_one_tiles(*pieces[5])
     level_one_product((1, 2))
@@ -551,11 +613,16 @@
                 q[corner, 4 + 2 * j:4 + 2 * j + size, :] = l3[0, row + first3:row + first3 + size, :]
 
 
-    for_neighbours(start, (2,), only=[d for d in LOWER if not d[2]])
+    for_neighbours(start, (2,), only=NEAR_LOWER)
     wait_for(ready.at[0], near_upper)
-    for_neighbours(start, only=[d for d in UPPER if d[2] == 0])
+    for_neighbours(start, (3,), only=NEAR_UPPER)
+    for_neighbours(start, (0, 1, 2), only=NEAR_UPPER)
     wait_for(ready.at[1], far_upper)
-    for_neighbours(start, only=[d for d in UPPER if d[2]])
+    for_neighbours(start, (2,), only=[NEXT])
+    settle(recv_sem.at[1], NEAR_LOWER, (3,), True)
+    for_neighbours(start, (4,), only=[NEXT])
+    settle(recv_sem.at[2], NEAR_UPPER, (3,), True)
+    for_neighbours(start, (5,), only=[NEXT])
 
     heights, depths = (32, 16, 8), (8, 4, 2)
     levels = (l1, l2, l3)
@@ -585,7 +652,7 @@
                 row = (p if dz == 1 else depth - 1) * height + (j if dy == 1 else height - 1)
                 add(level, t, slice(row, row + 1), value[p:p + 1])
 
-    for_neighbours(received, (0, 1, 2), back=True, only=[d for d in DIRECTIONS if d[1] and not d[2]])
+    settle(recv_sem.at[3], [d for d in DIRECTIONS if d[1] and not d[2]], (0, 1, 2), True)
     for dy in (1, -1):
         side = 0 if dy == 1 else 1
         for t in range(4):
@@ -600,7 +667,7 @@
             for t in range(2):
                 add_corner(dz, dy, 1, t, lambda j: rq[c, 8 + 4 * t + 2 * j:10 + 4 * t + 2 * j, :])
             add_corner(dz, dy, 2, 0, lambda j: rq[c, 4 + 2 * j:6 + 2 * j, :])
-    for_neighbours(received, (0, 1, 2), back=True, only=FACES[:2])
+    settle(recv_sem.at[4], FACES[:2], (0, 1, 2), True)
     for t in range(4):
         add_z(1, 0, t, lambda r: rz1[0, t, r:r + 8, :])
         add_z(-1, 0, t, lambda r: rz1[1, t, r:r + 8, :])
@@ -609,8 +676,9 @@
         add_z(-1, 1, t, lambda r: rz2d[t, r:r + 8, :])
     add_z(1, 2, 0, lambda r: rz3u[0, r:r + 8, :])
     add_z(-1, 2, 0, lambda r: rz3d[0, r:r + 8, :])
-    for_neighbours(sent)
-    for_neighbours(received, back=True, only=[d for d in DIRECTIONS if d[2]])
+    settle(send_sem.at[0], TARGETS, None, False)
+    settle(send_sem.at[1], NEAR_LOWER + NEAR_UPPER, (0, 1, 2), False)
+    settle(recv_sem.at[0], [NEXT] + FAR_LOWER, (2, 4, 5), True)
     third = lax.rem(lane, 3)
     low_lanes, high_lane = lane < 2, lane == 127
 
@@ -636,7 +704,7 @@
         add_columns(level, [(slice(row, row + 8), spread(value, g))])
     firsts = {0: 0, 1: 12, 2: 21}
     for dz, dy in SIDES:
-        value = both(rr[SIDE[dz, dy], 0], rr[SIDE[dz, dy], 1])
+        value = both(rru[SIDE[dz, dy]], rrd[SIDE[dz, dy]])
         for level in range(3):
             height, depth = heights[level], depths[level]
             if dy == 0:
@@ -723,10 +791,10 @@
             vmem(2, 8, LANES), vmem(2, 3, 8, LANES), vmem(4, 16, LANES),
             vmem(2, 4, 32, LANES), vmem(2, 32, LANES), vmem(2, 16, LANES), vmem(1, 16, LANES), vmem(1, 8, LANES),
             vmem(2, 4, 8, LANES), vmem(2, 3, 8, LANES), vmem(4, 16, LANES),
-            vmem(2, 8, LANES), vmem(8, 2, 8, LANES),
+            vmem(2, 8, LANES), vmem(8, 8, LANES), vmem(8, 8, LANES), vmem(8, 8, LANES),
             pltpu.SemaphoreType.DMA((6,)),
-            pltpu.SemaphoreType.DMA((26, 3)),
-            pltpu.SemaphoreType.DMA((26, 3)),
+            pltpu.SemaphoreType.DMA((2,)),
+            pltpu.SemaphoreType.DMA((5,)),
             pltpu.SemaphoreType.REGULAR((2,)),
         ],
         compiler_params=pltpu.CompilerParams(

time: 15.6 us -> 14.5 us (0.929)
  Pallas kernels: 14.8 us -> 13.6 us
    pallas_call x1, Pallas kernels: 14 us -> 12.8 us  [levels_of(): pl.pallas_call(functools.partial(pyramid, counts), out_shape=shapes, in_s...]
where the time goes in v4:
time: 14.5 us; the launch traced here: 14.2 us
  Pallas kernels  13.6 us (94%)
  between operations  0.64 us (4%)
    pallas_call x1, Pallas kernels, levels_of(): pl.pallas_call(functools.partial(pyramid, counts), out_shape=shapes, in_s...  12.8 us
    pallas_call x1, Pallas kernels, on_device(): pl.pallas_call(store, out_shape=shapes, in_specs=[pl.BlockSpec(memory_spa...  0.83 us

profile of v4, /device:TPU:235, one launch (start us, length us, event | category | flops | bytes accessed | tf_op | source)
XLA Modules:
  0.0 14.2 jit_solution(656711393806659178)
XLA Ops:
  0.6 12.8 %pyramid.1 = (f32[8,32,512]{2,1,0:T(8,128)S(1)}, f32[4,16,256]{2,1,0:T(8,128)S(1)}, f32[2,8,128]{2,1,0:T(8,128)S(1)}) custom-call(f32[16,64,1024]{2,1,0:T(8,128)} %vol.1), custom_call_target="tpu_custom_call" | custom-call | tf_op jit(solution)/shard_map/pyramid/pallas_call | solution.py:775
  13.4 0.8 %store.1 = (f32[8,32,512]{2,1,0:T(8,128)}, f32[4,16,256]{2,1,0:T(8,128)}, f32[2,8,128]{2,1,0:T(8,128)}) custom-call(f32[8,32,512]{2,1,0:T(8,128)S(1)} %get-tuple-element.6.in1, f32[4,16,256]{2,1,0:T(8,128)S(1)} %get-tuple-element.7.in2, f32[2,8,128]{2,1,0:T(8,128)S(1)} %get-tuple-element.8.in3), custom_call_target="tpu_custom_call" | custom-call | tf_op jit(solution)/shard_map/store/pallas_call | solution.py:762

commit v5 on v4

--- a/solution.py
+++ b/solution.py
@@ -275,7 +275,7 @@
 
     def awaited_with(d, stage):
         if d[2]:
-            return 0
+            return 5 if stage == 5 else 0
         if stage == 3:
             return 1 if d in NEAR_LOWER else 2
         return 3 if d[1] else 4
@@ -582,6 +582,16 @@
 
     combine(parts2, l2, 2, ROWS2, xflag)
     for_neighbours(start, (1,), only=LOWER)
+    prompt = (me["gx"] == counts["gx"] - 2) & (lax.rem(me["gz"], 2) == 0)
+
+    def pass_on():
+        wait_for(ready.at[0], near_upper)
+        for_neighbours(start, (3,), only=NEAR_UPPER)
+
+    @pl.when(prompt)
+    def _():
+        pass_on()
+
 
     for t in range(3):
         level_three_tile(l2.at[t], t)
@@ -614,8 +624,10 @@
 
 
     for_neighbours(start, (2,), only=NEAR_LOWER)
-    wait_for(ready.at[0], near_upper)
-    for_neighbours(start, (3,), only=NEAR_UPPER)
+    @pl.when(jnp.logical_not(prompt))
+    def _():
+        pass_on()
+
     for_neighbours(start, (0, 1, 2), only=NEAR_UPPER)
     wait_for(ready.at[1], far_upper)
     for_neighbours(start, (2,), only=[NEXT])
@@ -678,7 +690,7 @@
     add_z(-1, 2, 0, lambda r: rz3d[0, r:r + 8, :])
     settle(send_sem.at[0], TARGETS, None, False)
     settle(send_sem.at[1], NEAR_LOWER + NEAR_UPPER, (0, 1, 2), False)
-    settle(recv_sem.at[0], [NEXT] + FAR_LOWER, (2, 4, 5), True)
+    settle(recv_sem.at[0], [NEXT] + FAR_LOWER, (2, 4), True)
     third = lax.rem(lane, 3)
     low_lanes, high_lane = lane < 2, lane == 127
 
@@ -689,13 +701,15 @@
         moved = value if g == 0 else pltpu.roll(value, LANES - 3 * g, 1)
         return jnp.where(low_lanes, moved, 0.0), jnp.where(high_lane, moved, 0.0)
 
-    def add_columns(level, pairs):
+    def add_columns(level, pairs, keep=(True, True)):
         last = (3, 1, 0)[level]
         for rows, (low_value, high_value) in pairs:
-            if last == 0:
+            if last == 0 and keep == (True, True):
                 add(level, 0, rows, low_value + high_value)
-            else:
+                continue
+            if keep[0]:
                 add(level, 0, rows, low_value)
+            if keep[1]:
                 add(level, last, rows, high_value)
 
     value = both(rx[0], rx[1])
@@ -703,37 +717,44 @@
         level = 0 if g < 32 else (1 if g < 40 else 2)
         add_columns(level, [(slice(row, row + 8), spread(value, g))])
     firsts = {0: 0, 1: 12, 2: 21}
-    for dz, dy in SIDES:
-        value = both(rru[SIDE[dz, dy]], rrd[SIDE[dz, dy]])
-        for level in range(3):
-            height, depth = heights[level], depths[level]
-            if dy == 0:
-                first = firsts[level] + (height // 8 if dz == 1 else 0)
-                planes = 2 if dz == 1 and level else 1
-                to = 0 if dz == 1 else (depth - 1) * height
-                for r in range(planes * height // 8):
-                    add_columns(level, [(slice(to + 8 * r, to + 8 * r + 8), spread(value, first + r))])
-                continue
-            for j in range(2 if dy == 1 and level else 1):
-                y = j if dy == 1 else height - 1
-                if level == 0:
-                    group = (10 if dy == 1 else 8) + (1 if dz else 0)
-                else:
-                    group = {1: (18, 19), 2: (24, 25)}[level][1 if dy == 1 else 0] + j
-                parts = spread(value, group)
-                if dz == 0:
-                    if level:
-                        parts = tuple(x[1:1 + depth] for x in parts)
-                    add_columns(level, [(pl.ds(y, depth, stride=height), parts)])
+
+    def add_sides(sides, values, keep):
+        for dz, dy in sides:
+            value = values(SIDE[dz, dy])
+            for level in range(3):
+                height, depth = heights[level], depths[level]
+                if dy == 0:
+                    first = firsts[level] + (height // 8 if dz == 1 else 0)
+                    planes = 2 if dz == 1 and level else 1
+                    to = 0 if dz == 1 else (depth - 1) * height
+                    for r in range(planes * height // 8):
+                        add_columns(level, [(slice(to + 8 * r, to + 8 * r + 8), spread(value, first + r))], keep)
                     continue
-                for p in range(2 if dz == 1 and level else 1):
+                for j in range(2 if dy == 1 and level else 1):
+                    y = j if dy == 1 else height - 1
                     if level == 0:
-                        s = 1 if dz == 1 else 0
+                        group = (10 if dy == 1 else 8) + (1 if dz else 0)
                     else:
-                        s = depth + 1 + p if dz == 1 else 0
-                    z = p if dz == 1 else depth - 1
-                    row = slice(z * height + y, z * height + y + 1)
-                    add_columns(level, [(row, tuple(x[s:s + 1] for x in parts))])
+                        group = {1: (18, 19), 2: (24, 25)}[level][1 if dy == 1 else 0] + j
+                    parts = spread(value, group)
+                    if dz == 0:
+                        if level:
+                            parts = tuple(x[1:1 + depth] for x in parts)
+                        add_columns(level, [(pl.ds(y, depth, stride=height), parts)], keep)
+                        continue
+                    for p in range(2 if dz == 1 and level else 1):
+                        if level == 0:
+                            s = 1 if dz == 1 else 0
+                        else:
+                            s = depth + 1 + p if dz == 1 else 0
+                        z = p if dz == 1 else depth - 1
+                        row = slice(z * height + y, z * height + y + 1)
+                        add_columns(level, [(row, tuple(x[s:s + 1] for x in parts))], keep)
+
+    add_sides(SIDES[:4], lambda i: both(rru[i], rrd[i]), (True, True))
+    add_sides(SIDES[4:], lambda i: rrd[i], (False, True))
+    settle(recv_sem.at[5], [NEXT], (5,), True)
+    add_sides(SIDES[4:], lambda i: rru[i], (True, False))
 
     for z in range(8):
         for t in range(4):
@@ -794,7 +815,7 @@
             vmem(2, 8, LANES), vmem(8, 8, LANES), vmem(8, 8, LANES), vmem(8, 8, LANES),
             pltpu.SemaphoreType.DMA((6,)),
             pltpu.SemaphoreType.DMA((2,)),
-            pltpu.SemaphoreType.DMA((5,)),
+            pltpu.SemaphoreType.DMA((6,)),
             pltpu.SemaphoreType.REGULAR((2,)),
         ],
         compiler_params=pltpu.CompilerParams(

time: 14.5 us -> 14.3 us (0.986)
  Pallas kernels: 13.6 us -> 13.4 us
    pallas_call x1, Pallas kernels: 12.8 us -> 12.6 us  [levels_of(): pl.pallas_call(functools.partial(pyramid, counts), out_shape=shapes, in_s...]
where the time goes in v5:
time: 14.3 us; the launch traced here: 14.1 us
  Pallas kernels  13.4 us (94%)
  between operations  0.64 us (4%)
    pallas_call x1, Pallas kernels, levels_of(): pl.pallas_call(functools.partial(pyramid, counts), out_shape=shapes, in_s...  12.6 us
    pallas_call x1, Pallas kernels, on_device(): pl.pallas_call(store, out_shape=shapes, in_specs=[pl.BlockSpec(memory_spa...  0.83 us

profile of v5, /device:TPU:235, one launch (start us, length us, event | category | flops | bytes accessed | tf_op | source)
XLA Modules:
  0.0 14.1 jit_solution(16782955812383419155)
XLA Ops:
  0.6 12.6 %pyramid.1 = (f32[8,32,512]{2,1,0:T(8,128)S(1)}, f32[4,16,256]{2,1,0:T(8,128)S(1)}, f32[2,8,128]{2,1,0:T(8,128)S(1)}) custom-call(f32[16,64,1024]{2,1,0:T(8,128)} %vol.1), custom_call_target="tpu_custom_call" | custom-call | tf_op jit(solution)/shard_map/pyramid/pallas_call | solution.py:796
  13.2 0.8 %store.1 = (f32[8,32,512]{2,1,0:T(8,128)}, f32[4,16,256]{2,1,0:T(8,128)}, f32[2,8,128]{2,1,0:T(8,128)}) custom-call(f32[8,32,512]{2,1,0:T(8,128)S(1)} %get-tuple-element.6.in1, f32[4,16,256]{2,1,0:T(8,128)S(1)} %get-tuple-element.7.in2, f32[2,8,128]{2,1,0:T(8,128)S(1)} %get-tuple-element.8.in3), custom_call_target="tpu_custom_call" | custom-call | tf_op jit(solution)/shard_map/store/pallas_call | solution.py:783

commit v6 on v5

--- a/solution.py
+++ b/solution.py
@@ -278,7 +278,7 @@
             return 5 if stage == 5 else 0
         if stage == 3:
             return 1 if d in NEAR_LOWER else 2
-        return 3 if d[1] else 4
+        return (6 if d[0] else 3) if d[1] else 4
 
     def copies(d, stages=(0, 1, 2, 3, 4, 5)):
         return [
@@ -582,7 +582,7 @@
 
     combine(parts2, l2, 2, ROWS2, xflag)
     for_neighbours(start, (1,), only=LOWER)
-    prompt = (me["gx"] == counts["gx"] - 2) & (lax.rem(me["gz"], 2) == 0)
+    prompt = me["gx"] == counts["gx"] - 2
 
     def pass_on():
         wait_for(ready.at[0], near_upper)
@@ -664,7 +664,7 @@
                 row = (p if dz == 1 else depth - 1) * height + (j if dy == 1 else height - 1)
                 add(level, t, slice(row, row + 1), value[p:p + 1])
 
-    settle(recv_sem.at[3], [d for d in DIRECTIONS if d[1] and not d[2]], (0, 1, 2), True)
+    settle(recv_sem.at[3], FACES[2:], (0, 2), True)
     for dy in (1, -1):
         side = 0 if dy == 1 else 1
         for t in range(4):
@@ -672,13 +672,6 @@
         for t in range(2):
             add_y(dy, 1, t, lambda j: ryf[side, t, 4 * j:4 * j + 4, :])
         add_y(dy, 2, 0, lambda j: ryf[side, 2, 2 * j:2 * j + 2, :])
-        for dz in (1, -1):
-            c = CORNER[dz, dy]
-            for t in range(4):
-                add_corner(dz, dy, 0, t, lambda j: rq[c, t:t + 1, :])
-            for t in range(2):
-                add_corner(dz, dy, 1, t, lambda j: rq[c, 8 + 4 * t + 2 * j:10 + 4 * t + 2 * j, :])
-            add_corner(dz, dy, 2, 0, lambda j: rq[c, 4 + 2 * j:6 + 2 * j, :])
     settle(recv_sem.at[4], FACES[:2], (0, 1, 2), True)
     for t in range(4):
         add_z(1, 0, t, lambda r: rz1[0, t, r:r + 8, :])
@@ -753,6 +746,14 @@
 
     add_sides(SIDES[:4], lambda i: both(rru[i], rrd[i]), (True, True))
     add_sides(SIDES[4:], lambda i: rrd[i], (False, True))
+    settle(recv_sem.at[6], list(d + (0,) for d in CORNER), (2,), True)
+    for dz, dy in CORNER:
+        c = CORNER[dz, dy]
+        for t in range(4):
+            add_corner(dz, dy, 0, t, lambda j: rq[c, t:t + 1, :])
+        for t in range(2):
+            add_corner(dz, dy, 1, t, lambda j: rq[c, 8 + 4 * t + 2 * j:10 + 4 * t + 2 * j, :])
+        add_corner(dz, dy, 2, 0, lambda j: rq[c, 4 + 2 * j:6 + 2 * j, :])
     settle(recv_sem.at[5], [NEXT], (5,), True)
     add_sides(SIDES[4:], lambda i: rru[i], (True, False))
 
@@ -815,7 +816,7 @@
             vmem(2, 8, LANES), vmem(8, 8, LANES), vmem(8, 8, LANES), vmem(8, 8, LANES),
             pltpu.SemaphoreType.DMA((6,)),
             pltpu.SemaphoreType.DMA((2,)),
-            pltpu.SemaphoreType.DMA((6,)),
+            pltpu.SemaphoreType.DMA((7,)),
             pltpu.SemaphoreType.REGULAR((2,)),
         ],
         compiler_params=pltpu.CompilerParams(

time: 14.3 us -> 14 us (0.979)
  the two profiles are of different devices: /device:TPU:235 before, /device:TPU:233 now
where the time goes in v6:
time: 14 us; the launch traced here: 13.9 us
  Pallas kernels  13.3 us (95%)
  between operations  0.64 us (5%)
    pallas_call x1, Pallas kernels, levels_of(): pl.pallas_call(functools.partial(pyramid, counts), out_shape=shapes, in_s...  12.5 us
    pallas_call x1, Pallas kernels, on_device(): pl.pallas_call(store, out_shape=shapes, in_specs=[pl.BlockSpec(memory_spa...  0.83 us

profile of v6, /device:TPU:233, one launch (start us, length us, event | category | flops | bytes accessed | tf_op | source)
XLA Modules:
  0.0 13.9 jit_solution(10914755573185895156)
XLA Ops:
  0.6 12.5 %pyramid.1 = (f32[8,32,512]{2,1,0:T(8,128)S(1)}, f32[4,16,256]{2,1,0:T(8,128)S(1)}, f32[2,8,128]{2,1,0:T(8,128)S(1)}) custom-call(f32[16,64,1024]{2,1,0:T(8,128)} %vol.1), custom_call_target="tpu_custom_call" | custom-call | tf_op jit(solution)/shard_map/pyramid/pallas_call | solution.py:797
  13.1 0.8 %store.1 = (f32[8,32,512]{2,1,0:T(8,128)}, f32[4,16,256]{2,1,0:T(8,128)}, f32[2,8,128]{2,1,0:T(8,128)}) custom-call(f32[8,32,512]{2,1,0:T(8,128)S(1)} %get-tuple-element.6.in1, f32[4,16,256]{2,1,0:T(8,128)S(1)} %get-tuple-element.7.in2, f32[2,8,128]{2,1,0:T(8,128)S(1)} %get-tuple-element.8.in3), custom_call_target="tpu_custom_call" | custom-call | tf_op jit(solution)/shard_map/store/pallas_call | solution.py:784

commit v7 on v6

--- a/solution.py
+++ b/solution.py
@@ -570,6 +570,17 @@
 
     combine(parts1, l1, 4, ROWS1, xflag)
     for_neighbours(start, (0,), only=LOWER)
+    even = lax.rem(me["gz"], 2) == 0
+    prompt = me["gx"] == counts["gx"] - 2
+
+    def pass_on():
+        wait_for(ready.at[0], near_upper)
+        for_neighbours(start, (3,), only=NEAR_UPPER)
+
+    @pl.when(prompt & even)
+    def _():
+        pass_on()
+
     for t in range(5):
         level_two_tile(l1.at[t], t)
     for b in range(2):
@@ -582,16 +593,10 @@
 
     combine(parts2, l2, 2, ROWS2, xflag)
     for_neighbours(start, (1,), only=LOWER)
-    prompt = me["gx"] == counts["gx"] - 2
-
-    def pass_on():
-        wait_for(ready.at[0], near_upper)
-        for_neighbours(start, (3,), only=NEAR_UPPER)
-
-    @pl.when(prompt)
+
+    @pl.when(prompt & jnp.logical_not(even))
     def _():
         pass_on()
-
 
     for t in range(3):
         level_three_tile(l2.at[t], t)

time: 14 us -> 13.7 us (0.979)
  the two profiles are of different devices: /device:TPU:233 before, /device:TPU:235 now
where the time goes in v7:
time: 13.7 us; the launch traced here: 13.6 us
  Pallas kernels  12.9 us (94%)
  between operations  0.64 us (5%)
    pallas_call x1, Pallas kernels, levels_of(): pl.pallas_call(functools.partial(pyramid, counts), out_shape=shapes, in_s...  12.1 us
    pallas_call x1, Pallas kernels, on_device(): pl.pallas_call(store, out_shape=shapes, in_specs=[pl.BlockSpec(memory_spa...  0.83 us

profile of v7, /device:TPU:235, one launch (start us, length us, event | category | flops | bytes accessed | tf_op | source)
XLA Modules:
  0.0 13.6 jit_solution(16544298489992452368)
XLA Ops:
  0.6 12.1 %pyramid.1 = (f32[8,32,512]{2,1,0:T(8,128)S(1)}, f32[4,16,256]{2,1,0:T(8,128)S(1)}, f32[2,8,128]{2,1,0:T(8,128)S(1)}) custom-call(f32[16,64,1024]{2,1,0:T(8,128)} %vol.1), custom_call_target="tpu_custom_call" | custom-call | tf_op jit(solution)/shard_map/pyramid/pallas_call | solution.py:802
  12.7 0.8 %store.1 = (f32[8,32,512]{2,1,0:T(8,128)}, f32[4,16,256]{2,1,0:T(8,128)}, f32[2,8,128]{2,1,0:T(8,128)}) custom-call(f32[8,32,512]{2,1,0:T(8,128)S(1)} %get-tuple-element.6.in1, f32[4,16,256]{2,1,0:T(8,128)S(1)} %get-tuple-element.7.in2, f32[2,8,128]{2,1,0:T(8,128)S(1)} %get-tuple-element.8.in3), custom_call_target="tpu_custom_call" | custom-call | tf_op jit(solution)/shard_map/store/pallas_call | solution.py:789
